TPU v7x, 32 devices: a whole 2x2x4 slice. The times are simulated.
32 devices in a mesh: fsdp: 4 (over y, core), heads: 2 (over x), tensor: 4 (over z).
Axes of the slice: x: 2, y: 2, z: 4, core: 2. Of those that a mesh axis runs over, the one named last changes fastest.
Arguments:
- tokens: bfloat16 [64, 197, 512], P(('fsdp', 'tensor')), may hold values from -6 to 6
- cotangent: bfloat16 [64, 197, 512], P(('fsdp', 'tensor')), may hold values from -6 to 6
- w_qkv: bfloat16 [3, 512, 512], P(None, ('fsdp', 'tensor'), 'heads'), may hold values from -0.25 to 0.25
- w_out: bfloat16 [512, 512], P('heads', ('fsdp', 'tensor')), may hold values from -0.75 to 0.75
- w_router: bfloat16 [512, 32], P(('fsdp', 'tensor')), may hold values from -0.25 to 0.25
- norm_one: bfloat16 [512], P(('fsdp', 'tensor')), may hold values from 0.099609375 to 1.8984375
- norm_two: bfloat16 [512], P(('fsdp', 'tensor')), may hold values from 0.099609375 to 1.8984375
- w_in: bfloat16 [32, 512, 2048], P('heads', 'fsdp', 'tensor'), may hold values from -0.25 to 0.25
- w_back: bfloat16 [32, 2048, 512], P('heads', 'tensor', 'fsdp'), may hold values from -4 to 4
- routes: int32 [64, 197, 2], P(('fsdp', 'tensor')), may hold values from 0 to 31, all different within a row; in each aligned block of 788 rows (0 to 787, 788 to 1575, ..., all dimensions but the last counted through in order) at most 64 rows name the same one
Outputs:
- output: bfloat16 [64, 197, 512], P(('fsdp', 'tensor'))
- token_grad: float32 [64, 197, 512], P(('fsdp', 'tensor'))
- qkv_grad: float32 [3, 512, 512], P(None, ('fsdp', 'tensor'), 'heads')
- out_grad: float32 [512, 512], P('heads', ('fsdp', 'tensor'))
- router_grad: float32 [512, 32], P(('fsdp', 'tensor'))
- norm_one_grad: float32 [512], P(('fsdp', 'tensor'))
- norm_two_grad: float32 [512], P(('fsdp', 'tensor'))
- in_grad: float32 [32, 512, 2048], P('heads', 'fsdp', 'tensor')
- back_grad: float32 [32, 2048, 512], P('heads', 'tensor', 'fsdp')
Inputs may be any that keep to these rules, and one draw needn't show every extreme that they name: Each token names two different experts. Within the 788 tokens of one group (aligned blocks of rows), no expert is named by more than 64 routes, a bound that some block reaches.
All inputs are finite; a program needn't handle non-finite values.
Results may differ from a plain program's by a relative error of at most 0.02.
Values may be sent and summed in bfloat16 or wider, within the bound.
A program may use at most 192 MiB of HBM per device.

v0:
```python
import functools

import jax
import jax.numpy as jnp
from jax import lax
from jax.experimental import pallas as pl
from jax.experimental.pallas import tpu as pltpu
from jax.sharding import PartitionSpec as P

HD = 64
EXPERTS = 32
CAP = 64
PAIR = 2
LANES = 128
MESH = pl.DeviceIdType.MESH
F32 = jnp.float32
BF16 = jnp.bfloat16


def mm(a, b):
    return lax.dot_general(a, b, (((1,), (0,)), ((), ())), preferred_element_type=F32)


def mm_nt(a, b):
    return lax.dot_general(a, b, (((1,), (1,)), ((), ())), preferred_element_type=F32)


def mm_tn(a, b):
    return lax.dot_general(a, b, (((0,), (0,)), ((), ())), preferred_element_type=F32)


def iota(shape, dim):
    return lax.broadcasted_iota(jnp.int32, shape, dim).astype(F32)


def norm_of(x):
    centre = x - jnp.mean(x, axis=-1, keepdims=True)
    spread = lax.rsqrt(jnp.mean(centre * centre, axis=-1, keepdims=True) + 1e-06)
    return centre * spread, spread


def norm_back(scaled, normed, spread):
    middle = jnp.mean(scaled, axis=-1, keepdims=True)
    along = jnp.mean(scaled * normed, axis=-1, keepdims=True)
    return spread * (scaled - middle - normed * along)


class Sizes:
    def __init__(self, mesh_shape, images, length, width, home, ff_shard):
        self.tensor = mesh_shape["tensor"]
        self.heads = mesh_shape["heads"]
        self.pair = PAIR if self.tensor % PAIR == 0 else 1
        self.halves = self.tensor // self.pair
        self.team_i = min(mesh_shape["fsdp"], max(1, home // self.tensor))
        self.reps = mesh_shape["fsdp"] // self.team_i
        self.team = self.team_i * self.tensor
        self.home = home
        self.own_e = home // (self.team_i * self.pair)
        self.images = images
        self.length = length
        self.width = width
        self.pad = -(-length // 16) * 16
        self.own_img = images // self.heads
        self.own = self.own_img * self.pad
        self.all = images * self.pad
        self.rows = -(-self.all // LANES) * LANES
        self.ffs = ff_shard
        self.ff = ff_shard * self.pair
        self.slots = home * CAP
        self.dq = width // self.team_i
        self.wrow = self.dq // self.tensor
        self.ecols = width // self.heads
        self.lw = self.own_e * CAP
        self.nh = width // HD


def kernel(z, names, *refs):
    ref = dict(zip(names, refs))
    tok, cot, rt, wpack, spack = ref["tok"], ref["cot"], ref["rt"], ref["wpack"], ref["spack"]
    win, wback = ref["win"], ref["wback"]
    T, I, R = z.tensor, z.team_i, z.reps
    D, L, RP = z.width, z.length, z.pad
    OWN, ALL, ROWS = z.own, z.all, z.rows
    PR, A, ED = z.pair, z.halves, z.own_e
    FS, DQ, WR, EC = z.ffs, z.dq, z.wrow, z.ecols

    fs, h, t = lax.axis_index("fsdp"), lax.axis_index("heads"), lax.axis_index("tensor")
    i, r = fs // R, lax.rem(fs, R)
    oh = 1 - h
    pos, half = lax.rem(t, PR), t // PR
    e0 = (i * PR + pos) * ED
    i_core = i + 1 - 2 * lax.rem(i, 2)
    i_far = lax.rem(i + 2, I)
    i_diag = lax.rem(i_core + 2, I)
    mine = i * T + t

    def dev(ii, tt, hh=None):
        return {"fsdp": ii * R + r, "heads": h if hh is None else hh, "tensor": tt}

    def rcopy(src, dst, ssem, rsem, target):
        return pltpu.make_async_remote_copy(
            src_ref=src, dst_ref=dst, send_sem=ssem, recv_sem=rsem, device_id=target, device_id_type=MESH
        )

    def lcopy(src, dst, sem):
        return pltpu.make_async_copy(src, dst, sem)

    def al(v, m):
        return pl.multiple_of(v, m)

    bar = pltpu.get_barrier_semaphore()
    for di in range(I):
        for dt in range(T):
            if di or dt:
                pl.semaphore_signal(
                    bar, inc=1, device_id=dev(lax.rem(i + di, I), lax.rem(t + dt, T)), device_id_type=MESH
                )
    pl.semaphore_signal(bar, inc=1, device_id=dev(i, t, oh), device_id_type=MESH)
    pl.semaphore_wait(bar, I * T)

    wall, sall = ref["wall"], ref["sall"]
    ws, wr, wl = ref["ws"], ref["wr"], ref["wl"]

    def shard_of(buf):
        return buf.at[:, pl.ds(al(mine * WR, WR), WR), pl.ds(al(h * EC, LANES), EC)]

    def block(buf, ii, hh):
        return buf.at[:, pl.ds(al(ii * DQ, DQ), DQ), pl.ds(al(hh * EC, LANES), EC)]

    def srows(ii):
        return sall.at[pl.ds(al(ii * DQ, DQ), DQ)]

    s_mine = sall.at[pl.ds(al(mine * WR, WR), WR)]
    first = []
    for dt in range(1, T):
        to = dev(i, lax.rem(t + dt, T))
        first.append(rcopy(wpack, shard_of(wall), ws.at[0, dt], wr.at[0, dt], to))
        first.append(rcopy(spack, s_mine, ws.at[1, dt], wr.at[1, dt], to))
    for c in first:
        c.start()
    own_w = [lcopy(wpack, shard_of(wall), wl.at[0]), lcopy(spack, s_mine, wl.at[1])]
    for c in own_w:
        c.start()

    xn2a, cota, rp = ref["xn2a"], ref["cota"], ref["rp"]
    xn2a[...] = jnp.zeros_like(xn2a)
    cota[...] = jnp.zeros_like(cota)
    rp[...] = jnp.full_like(rp, -1.0)
    xs = ref["xs"]
    xs[...] = jnp.zeros_like(xs)
    for m in range(z.images):
        cota[pl.ds(m * RP, L), :] = cot[m]
        rp[pl.ds(m * RP, L), 0:2] = rt[m].astype(F32)
    for m in range(z.own_img):
        xs[pl.ds(m * RP, L), :] = tok[h * z.own_img + m].astype(F32)

    lane_all = iota((ROWS, LANES), 1)
    r0, r1 = rp[:, 0:1], rp[:, 1:2]
    oh0 = jnp.where(r0 == lane_all, 1.0, 0.0)
    oh1 = jnp.where(r1 == lane_all, 1.0, 0.0)
    both = ref["both"]
    both[...] = (oh0 + oh1).astype(BF16)
    idc = ref["idc"]

    def count(c, _):
        at = pl.ds(al(c * LANES, LANES), LANES)
        before = iota((LANES, ROWS), 1) < iota((LANES, ROWS), 0) + (c * LANES).astype(F32)
        counted = mm(jnp.where(before, 1.0, 0.0).astype(BF16), both[...])
        lane = iota((LANES, LANES), 1)
        q0, q1 = rp[at, 0:1], rp[at, 1:2]
        number = counted + lane * CAP
        n0 = jnp.sum(jnp.where(q0 == lane, number, 0.0), axis=1, keepdims=True)
        n1 = jnp.sum(jnp.where(q1 == lane, number, 0.0), axis=1, keepdims=True)
        n0 = jnp.where(q0 < 0.0, -1.0, n0)
        n1 = jnp.where(q1 < 0.0, -1.0, n1)
        idc[at, :] = jnp.where(lane == 0.0, n0, jnp.where(lane == 1.0, n1, -1.0))
        return 0

    lax.fori_loop(0, ROWS // LANES, count, 0)
    idr = ref["idr"]
    idr[...] = jnp.transpose(idc[...])

    gs, xsl = ref["gs"], ref["xsl"]

    def dispatch(source, target):
        def one(c, _):
            slot = iota((LANES, ROWS), 0) + (c * LANES + h * z.slots).astype(F32)
            pick = jnp.where(idr[0:1, :] == slot, 1.0, 0.0) + jnp.where(idr[1:2, :] == slot, 1.0, 0.0)
            got = mm(pick.astype(BF16), source[...]).astype(BF16)
            per = LANES // CAP
            target[pl.ds(c * per, per)] = got.reshape(per, CAP, D)
            return 0

        lax.fori_loop(0, z.slots // LANES, one, 0)

    dispatch(cota, gs)

    for c in first:
        c.wait_recv()
    for c in own_w:
        c.wait()
    b_x = rcopy(block(wall, i, h), block(wall, i, h), ws.at[2, 0], wr.at[2, 0], dev(i, t, oh))
    b_y = rcopy(block(wall, i, h), block(wall, i, h), ws.at[2, 1], wr.at[2, 1], dev(i_far, t))
    b_ys = rcopy(srows(i), srows(i), ws.at[2, 2], wr.at[2, 2], dev(i_far, t))
    b_c = rcopy(block(wall, i, h), block(wall, i, h), ws.at[2, 3], wr.at[2, 3], dev(i_core, t))
    b_cs = rcopy(srows(i), srows(i), ws.at[3, 0], wr.at[3, 0], dev(i_core, t))
    for c in (b_y, b_x, b_ys, b_c, b_cs):
        c.start()
    b_y.wait_recv()
    f_x = rcopy(block(wall, i_far, h), block(wall, i_far, h), ws.at[3, 1], wr.at[3, 1], dev(i, t, oh))
    f_x.start()
    f_c = rcopy(block(wall, i_far, h), block(wall, i_far, h), ws.at[3, 2], wr.at[3, 2], dev(i_core, t))
    f_c.start()
    b_ys.wait_recv()
    f_cs = rcopy(srows(i_far), srows(i_far), ws.at[3, 3], wr.at[3, 3], dev(i_core, t))
    f_cs.start()
    b_x.wait_recv()
    f_c2 = rcopy(block(wall, i, oh), block(wall, i, oh), ws.at[4, 0], wr.at[4, 0], dev(i_core, t))
    f_c2.start()

    vin, vback = ref["vin"], ref["vback"]
    es, er = ref["es"], ref["er"]
    moved = []
    k = 0
    for dp in range(PR):
        for di in range(I):
            ii, pp = lax.rem(i + di, I), lax.rem(pos + dp, PR)
            them = pl.ds((ii * PR + pp) * ED, ED)
            to_in = vin.at[:, pl.ds(al(i * DQ, DQ), DQ), pl.ds(al(pos * FS, FS), FS)]
            to_back = vback.at[:, pl.ds(al(pos * FS, FS), FS), pl.ds(al(i * DQ, DQ), DQ)]
            if di == 0 and dp == 0:
                moved.append(lcopy(win.at[them], to_in, er.at[0, 0]))
                moved.append(lcopy(wback.at[them], to_back, er.at[1, 0]))
            else:
                to = dev(ii, half * PR + pp)
                moved.append(rcopy(win.at[them], to_in, es.at[0, k], er.at[0, k], to))
                moved.append(rcopy(wback.at[them], to_back, es.at[1, k], er.at[1, k], to))
            k += 1
    for c in moved:
        c.start()

    xr, gr, gater = ref["xr"], ref["gr"], ref["gater"]
    ds, dr = ref["ds"], ref["dr"]

    def spread(src, dst, row, whole):
        made = []
        for di in range(I):
            for dt in range(T):
                kk = di * T + dt
                ii, tt = lax.rem(i + di, I), lax.rem(t + dt, T)
                pp = lax.rem(tt, PR)
                if whole:
                    s, d = src.at[ii * PR + pp], dst.at[mine]
                else:
                    s, d = src.at[pl.ds((ii * PR + pp) * ED, ED)], dst.at[:, mine]
                if kk == 0:
                    made.append(lcopy(s, d, dr.at[row, 0]))
                else:
                    made.append(rcopy(s, d, ds.at[row, kk], dr.at[row, kk], dev(ii, tt)))
        for c in made:
            c.start()
        return made

    g_moved = spread(gs, gr, 0, False)

    f_x.wait_recv()
    f_c3 = rcopy(block(wall, i_far, oh), block(wall, i_far, oh), ws.at[4, 1], wr.at[4, 1], dev(i_core, t))
    f_c3.start()
    for c in (b_c, b_cs, f_c, f_cs, f_c2, f_c3):
        c.wait_recv()

    sall_t = jnp.transpose(sall[...].astype(F32))
    gains = ref["gains"]
    gains[...] = sall_t[EXPERTS : EXPERTS + 8, :]
    xn1, qkv, mixed, probs = ref["xn1"], ref["qkv"], ref["mixed"], ref["probs"]
    normed, _ = norm_of(xs[...])
    xn1[...] = (normed * gains[0:1, :]).astype(BF16)

    def project(j, _):
        qkv[j] = mm(xn1[...], wall[j]).astype(BF16)
        return 0

    lax.fori_loop(0, 3, project, 0)
    groups = D // LANES
    scale = HD ** (-0.5)

    def attend(n, _):
        rows = pl.ds(al((n // groups) * RP, 16), RP)
        cols = pl.ds(al(lax.rem(n, groups) * LANES, LANES), LANES)
        q, kk, v = qkv[0, rows, cols], qkv[1, rows, cols], qkv[2, rows, cols]
        low = iota((RP, LANES), 1) < HD
        key = iota((RP, RP), 1)
        outs = []
        for s in range(2):
            sel = low if s == 0 else jnp.logical_not(low)
            score = mm_nt(jnp.where(sel, q, jnp.zeros_like(q)), kk) * scale
            score = jnp.where(key < L, score, -1e30)
            e = jnp.exp(score - jnp.max(score, axis=-1, keepdims=True))
            p = e / jnp.sum(e, axis=-1, keepdims=True)
            p = p.astype(BF16)
            probs[n * 2 + s] = p
            outs.append(mm(p, v))
        mixed[rows, cols] = jnp.where(low, outs[0], outs[1]).astype(BF16)
        return 0

    lax.fori_loop(0, z.own_img * groups, attend, 0)
    resid = ref["resid"]
    resid[...] = xs[...] + mm_nt(mixed[...], wall[3])
    normed, _ = norm_of(resid[...])
    mine_rows = pl.ds(al(h * OWN, 16), OWN)
    other_rows = pl.ds(al(oh * OWN, 16), OWN)
    xn2a[mine_rows, :] = (normed * gains[1:2, :]).astype(BF16)

    xsm, xrm = ref["xsm"], ref["xrm"]
    x_swap = rcopy(xn2a.at[mine_rows], xn2a.at[mine_rows], xsm.at[0], xrm.at[0], dev(i, t, oh))
    x_swap.start()
    x_swap.wait_recv()
    logits = mm(xn2a[...], sall[...])
    logits = jnp.where(lane_all < EXPERTS, logits, -1e30)
    e = jnp.exp(logits - jnp.max(logits, axis=-1, keepdims=True))
    router = ref["router"]
    router[...] = e / jnp.sum(e, axis=-1, keepdims=True)
    gcol = ref["gcol"]
    g0 = jnp.sum(jnp.where(rp[:, 0:1] == lane_all, router[...], 0.0), axis=1, keepdims=True)
    g1 = jnp.sum(jnp.where(rp[:, 1:2] == lane_all, router[...], 0.0), axis=1, keepdims=True)
    gcol[...] = jnp.where(lane_all == 0.0, g0, g1)
    dispatch(xn2a, xsl)
    x_moved = spread(xsl, xr, 1, False)
    gsend = ref["gsend"]

    def gate_row(c, _):
        lane = lane_all + (c * z.lw + h * z.slots).astype(F32)
        keep = lane_all < z.lw
        w = jnp.where(jnp.logical_and(keep, idc[:, 0:1] == lane), gcol[:, 0:1], 0.0)
        w = w + jnp.where(jnp.logical_and(keep, idc[:, 1:2] == lane), gcol[:, 1:2], 0.0)
        gsend[c] = jnp.broadcast_to(jnp.sum(w, axis=0, keepdims=True), (8, LANES))
        return 0

    lax.fori_loop(0, z.home // ED, gate_row, 0)
    gate_moved = spread(gsend, gater, 2, True)

    hid, igs, gtile = ref["hid"], ref["igs"], ref["gtile"]
    eoa, sia = ref["eoa"], ref["sia"]
    eos, sis, ggs = ref["eos"], ref["sis"], ref["ggs"]
    eor, sir, ggr = ref["eor"], ref["sir"], ref["ggr"]
    rs, rr = ref["rs"], ref["rr"]
    gcols = ref["gcols"]
    ggs[...] = jnp.zeros_like(ggs)
    for c in moved:
        c.wait()
    TR = T * CAP
    eye = iota((LANES, LANES), 0) == iota((LANES, LANES), 1)

    def wait_role(row, kk, dst):
        pltpu.make_async_copy(dst, dst, dr.at[row, kk]).wait()

    def tile(n, _):
        gi = lax.rem(i - n + I, I)
        grp = pl.ds(gi * T, T)
        for dt in range(T):
            src = gi * T + lax.rem(t - dt + T, T)
            wait_role(0, n * T + dt, gr.at[:, src])
            wait_role(1, n * T + dt, xr.at[:, src])
            wait_role(2, n * T + dt, gater.at[src])
        for dt in range(T):
            row = gater[gi * T + dt][0:1, :]
            col = jnp.sum(jnp.where(eye, jnp.broadcast_to(row, (LANES, LANES)), 0.0), axis=1, keepdims=True)
            gcols[dt] = jnp.broadcast_to(col, (LANES, LANES))

        def part(ep, _):
            e, p = ep // PR, lax.rem(ep, PR)
            cols = pl.ds(al(p * FS, FS), FS)
            trow = pl.ds(al(gi * TR, TR), TR)
            x = xr[e, grp].reshape(TR, D)

            @pl.when(p == 0)
            def _():
                g = gr[e, grp].reshape(TR, D)
                gtile[...] = g
                gate = gcols[:, pl.ds(al(e * CAP, CAP), CAP), :].reshape(TR, LANES)[:, 0:1]
                gr[e, grp] = (g.astype(F32) * gate).astype(BF16).reshape(T, CAP, D)
                eoa[...] = jnp.zeros_like(eoa)
                sia[...] = jnp.zeros_like(sia)

            inner = mm(x, vin[e, :, cols])
            erf = lax.erf(inner * (0.5**0.5))
            cdf = 0.5 * (1.0 + erf)
            hidden = (inner * cdf).astype(BF16)
            slope = cdf + inner * (jnp.exp(-0.5 * inner * inner) * 0.3989422804014327)
            hid[e, trow, cols] = hidden
            eoa[...] += mm(hidden, vback[e, cols, :])
            back = mm_nt(gr[e, grp].reshape(TR, D), vback[e, cols, :])
            inner_grad = (back * slope).astype(BF16)
            igs[e, trow, cols] = inner_grad
            sia[...] += mm_nt(inner_grad, vin[e, :, cols])

            @pl.when(p == PR - 1)
            def _():
                eo = eoa[...]
                eos[e, grp] = eo.astype(BF16).reshape(T, CAP, D)
                sis[e, grp] = sia[...].astype(BF16).reshape(T, CAP, D)
                gg = jnp.sum(eo * gtile[...].astype(F32), axis=1, keepdims=True)
                there = iota((CAP, LANES), 1) == iota((CAP, LANES), 0) + (e * CAP).astype(F32)
                for dt in range(T):
                    piece = jnp.broadcast_to(gg[dt * CAP : (dt + 1) * CAP], (CAP, LANES))
                    line = jnp.sum(jnp.where(there, piece, 0.0), axis=0, keepdims=True)
                    ggs[gi * T + dt] = ggs[gi * T + dt] + jnp.broadcast_to(line, (8, LANES))

            return 0

        lax.fori_loop(0, ED * PR, part, 0)
        give_back(n, 0, sis, sir, False)
        give_back(n, 2, ggs, ggr, True)
        return 0

    def give_back(n, row, src, dst, whole):
        gi = lax.rem(i - n + I, I)
        for dt in range(T):
            tt = lax.rem(t + dt, T)
            kk = n * T + dt
            if whole:
                s, d = src.at[gi * T + tt], dst.at[mine]
            else:
                s, d = src.at[:, gi * T + tt], dst.at[half, pl.ds(e0, ED)]
            if dt == 0:

                @pl.when(n == 0)
                def _():
                    lcopy(s, d, rr.at[row, kk]).start()

                @pl.when(n > 0)
                def _():
                    rcopy(s, d, rs.at[row, kk], rr.at[row, kk], dev(gi, tt)).start()

            else:
                rcopy(s, d, rs.at[row, kk], rr.at[row, kk], dev(gi, tt)).start()

    lax.fori_loop(0, I, tile, 0)

    def give_eo(n, _):
        give_back(n, 1, eos, eor, False)
        return 0

    lax.fori_loop(0, I, give_eo, 0)

    ing, backg = ref["ing"], ref["backg"]
    vs, vr = ref["vs"], ref["vr"]

    def weight_grad(ep, _):
        e, p = ep // PR, lax.rem(ep, PR)
        cols = pl.ds(al(p * FS, FS), FS)
        vin[e, :, cols] = mm_tn(xr[e].reshape(z.team * CAP, D), igs[e, :, cols]).astype(BF16)
        vback[e, cols, :] = mm_tn(hid[e, :, cols], gr[e].reshape(z.team * CAP, D)).astype(BF16)
        for di in range(I):
            ii = lax.rem(i + di, I)
            part_in = vin.at[e, pl.ds(al(ii * DQ, DQ), DQ), cols]
            part_back = vback.at[e, cols, pl.ds(al(ii * DQ, DQ), DQ)]
            to_in, to_back = ing.at[e0 + e], backg.at[e0 + e]
            if di == 0:

                @pl.when(p == pos)
                def _():
                    lcopy(part_in, to_in, vr.at[0, e0 + e]).start()
                    lcopy(part_back, to_back, vr.at[1, e0 + e]).start()

                @pl.when(p != pos)
                def _():
                    rcopy(part_in, to_in, vs.at[0, ep * I], vr.at[0, e0 + e], dev(ii, half * PR + p)).start()
                    rcopy(part_back, to_back, vs.at[1, ep * I], vr.at[1, e0 + e], dev(ii, half * PR + p)).start()

            else:
                to = dev(ii, half * PR + p)
                rcopy(part_in, to_in, vs.at[0, ep * I + di], vr.at[0, e0 + e], to).start()
                rcopy(part_back, to_back, vs.at[1, ep * I + di], vr.at[1, e0 + e], to).start()
        return 0

    lax.fori_loop(0, ED * PR, weight_grad, 0)

    ggx = ref["ggx"]
    cacc = ref["cacc"]

    def from_of(n, dt):
        return lax.rem(i + n, I), lax.rem(t - dt + T, T)

    def wait_home(row, view):
        def one(n, _):
            for dt in range(T):
                fi, ft = from_of(n, dt)
                d = view(fi, ft)
                pltpu.make_async_copy(d, d, rr.at[row, n * T + dt]).wait()
            return 0

        lax.fori_loop(0, I, one, 0)

    def slot_view(buf):
        return lambda fi, ft: buf.at[ft // PR, pl.ds((fi * PR + lax.rem(ft, PR)) * ED, ED)]

    wait_home(2, lambda fi, ft: ggr.at[fi * T + ft])
    gg_swap = rcopy(ggr, ggx, xsm.at[1], xrm.at[1], dev(i, t, oh))
    gg_swap.start()
    wait_home(0, slot_view(sir))

    CH = 256

    def combine(rows, src, weighted):
        c0, c1 = idc[rows, 0:1], idc[rows, 1:2]
        w0 = gcol[rows, 0:1] if weighted else 1.0
        w1 = gcol[rows, 1:2] if weighted else 1.0
        cacc[...] = jnp.zeros_like(cacc)

        def one(c, _):
            lane = iota((OWN, CH), 1) + (c * CH + h * z.slots).astype(F32)
            w = jnp.where(c0 == lane, w0, 0.0) + jnp.where(c1 == lane, w1, 0.0)
            w = w.astype(BF16)
            for a in range(A):
                cacc[...] += mm(w, src[a, pl.ds(c * (CH // CAP), CH // CAP)].reshape(CH, D))
            return 0

        lax.fori_loop(0, z.slots // CH, one, 0)

    dbs, dbr = ref["dbs"], ref["dbr"]
    combine(other_rows, sir, False)
    dbs[...] = cacc[...].astype(BF16)
    db_swap = rcopy(dbs, dbr, xsm.at[2], xrm.at[2], dev(i, t, oh))
    db_swap.start()
    combine(mine_rows, sir, False)

    lane_own = iota((OWN, LANES), 1)
    m0, m1 = rp[mine_rows, 0:1], rp[mine_rows, 1:2]
    gg_swap.wait_recv()
    ggacc = ref["ggacc"]
    ggacc[...] = jnp.zeros_like(ggacc)

    def gate_back(q, _):
        fi, pp = q // PR, lax.rem(q, PR)
        k0, k1 = idc[mine_rows, 0:1], idc[mine_rows, 1:2]
        for buf, hh in ((ggr, h), (ggx, oh)):
            line = buf[fi * T + pp][0:1, :]
            for a in range(1, A):
                line = line + buf[fi * T + a * PR + pp][0:1, :]
            lane = lane_own + (q * z.lw + hh * z.slots).astype(F32)
            keep = lane_own < z.lw
            ggacc[0] += jnp.where(jnp.logical_and(keep, k0 == lane), line, 0.0)
            ggacc[1] += jnp.where(jnp.logical_and(keep, k1 == lane), line, 0.0)
        return 0

    lax.fori_loop(0, z.home // ED, gate_back, 0)
    gg0 = jnp.sum(ggacc[0], axis=1, keepdims=True)
    gg1 = jnp.sum(ggacc[1], axis=1, keepdims=True)
    mrouter = router[mine_rows, :]
    pgrad = jnp.where(m0 == lane_own, gg0, 0.0) + jnp.where(m1 == lane_own, gg1, 0.0)
    lgrad = (mrouter * (pgrad - jnp.sum(pgrad * mrouter, axis=1, keepdims=True))).astype(BF16)
    xn2 = xn2a[mine_rows, :]
    small = ref["small"]
    small[...] = jnp.where(iota((D, LANES), 1) < EXPERTS, mm_tn(xn2, lgrad), 0.0)
    through = mm_nt(lgrad, sall[...])
    db_swap.wait_recv()
    xgrad = cacc[...] + dbr[...].astype(F32) + through
    normed, spread_two = norm_of(resid[...])
    nrows = ref["nrows"]
    nrows[...] = jnp.zeros_like(nrows)
    nrows[EXPERTS + 1 : EXPERTS + 2, :] = jnp.sum(xgrad * normed, axis=0, keepdims=True)
    rgrad = ref["rgrad"]
    rgrad[...] = cota[mine_rows, :].astype(F32) + norm_back(xgrad * gains[1:2, :], normed, spread_two)

    agrad = rgrad[...].astype(BF16)

    def gw(j, row, count):
        return (0, pl.ds(al((j // 2) * D + row, LANES), count), pl.ds(al(lax.rem(j, 2) * D, LANES), D))

    hid[gw(jnp.int32(3), 0, D)] = mm_tn(agrad, mixed[...]).astype(BF16)
    mg = ref["mg"]
    mg[...] = mm(agrad, wall[3]).astype(BF16)
    pg = ref["pg"]

    def attend_back(n, _):
        rows = pl.ds(al((n // groups) * RP, 16), RP)
        cols = pl.ds(al(lax.rem(n, groups) * LANES, LANES), LANES)
        q, kk, v = qkv[0, rows, cols], qkv[1, rows, cols], qkv[2, rows, cols]
        m = mg[rows, cols]
        low = iota((RP, LANES), 1) < HD
        dq, dk, dv = [], [], []
        for s in range(2):
            sel = low if s == 0 else jnp.logical_not(low)
            low_p = probs[n * 2 + s]
            p = low_p.astype(F32)
            dp = mm_nt(jnp.where(sel, m, jnp.zeros_like(m)), v)
            dv.append(mm_tn(low_p, m))
            sg = (p * (dp - jnp.sum(dp * p, axis=-1, keepdims=True))).astype(BF16)
            dq.append(mm(sg, kk))
            dk.append(mm_tn(sg, q))
        pg[0, rows, cols] = (jnp.where(low, dq[0], dq[1]) * scale).astype(BF16)
        pg[1, rows, cols] = (jnp.where(low, dk[0], dk[1]) * scale).astype(BF16)
        pg[2, rows, cols] = jnp.where(low, dv[0], dv[1]).astype(BF16)
        return 0

    lax.fori_loop(0, z.own_img * groups, attend_back, 0)
    cacc[...] = jnp.zeros_like(cacc)

    def project_back(j, _):
        hid[gw(j, 0, D)] = mm_tn(xn1[...], pg[j]).astype(BF16)
        cacc[...] += mm_nt(pg[j], wall[j])
        return 0

    lax.fori_loop(0, 3, project_back, 0)

    s1r, s2s, s2r, s3s, s3r, s4s, s4r = (ref[n] for n in ("s1r", "s2s", "s2r", "s3s", "s3r", "s4s", "s4r"))
    u1s, u1r, u3s, u3r, u4s, u4r, u5s, u5r = (ref[n] for n in ("u1s", "u1r", "u3s", "u3r", "u4s", "u4r", "u5s", "u5r"))
    qs, qr = ref["qs"], ref["qr"]

    def quarter(ii):
        return pl.ds(al(ii * DQ, DQ), DQ)

    sw1 = []
    for b, ii in enumerate((i_core, i_diag)):
        for jr in range(2):
            src = hid.at[0, pl.ds(al(jr * D + ii * DQ, LANES), DQ), pl.ds(0, 2 * D)]
            sw1.append(rcopy(src, s1r.at[jr, b], qs.at[13 + 2 * b + jr], qr.at[13 + 2 * b + jr], dev(i_core, t)))
    for c in sw1:
        c.start()

    normed, spread_one = norm_of(xs[...])
    nrows[EXPERTS : EXPERTS + 1, :] = jnp.sum(cacc[...] * normed, axis=0, keepdims=True)
    tgrad = rgrad[...] + norm_back(cacc[...] * gains[0:1, :], normed, spread_one)
    tgs, tgr = ref["tgs"], ref["tgr"]
    tgs[...] = tgrad.astype(BF16)
    t_swap = rcopy(tgs, tgr, xsm.at[3], xrm.at[3], dev(i, t, oh))
    t_swap.start()
    small[...] = small[...] + jnp.transpose(nrows[...])
    for b, ii in enumerate((i_core, i_diag)):
        u1s[b] = small[quarter(ii), :]
    sv1 = rcopy(u1s, u1r, qs.at[1], qr.at[1], dev(i_core, t))
    sv1.start()
    for c in sw1:
        c.wait_recv()
    sv1.wait_recv()
    accu, acc2 = ref["accu"], ref["acc2"]
    for b, ii in enumerate((i, i_far)):
        for j in range(4):
            for hh, keep in ((oh, False), (h, True)):
                cols = pl.ds(al((j % 2) * D + hh * EC, LANES), EC)
                here = hid[0, pl.ds(al((j // 2) * D + ii * DQ, LANES), DQ), cols].astype(F32)
                here = here + s1r[j // 2, b, :, cols].astype(F32)
                if keep:
                    acc2[j, b] = here
                else:
                    s2s[j, b] = here.astype(BF16)
        accu[b] = small[quarter(ii), :] + u1r[b]
    sw2 = rcopy(s2s, s2r, qs.at[2], qr.at[2], dev(i, t, oh))
    sw2.start()
    u3s[...] = accu[1]
    sv3 = rcopy(u3s, u3r, qs.at[3], qr.at[3], dev(i_far, t))
    sv3.start()

    out_o, tg_o = ref["out_o"], ref["tg_o"]
    mos, mor, outs, outr = ref["mos"], ref["mor"], ref["outs"], ref["outr"]
    wait_home(1, slot_view(eor))
    combine(other_rows, eor, True)
    mos[...] = cacc[...].astype(BF16)
    m_swap = rcopy(mos, mor, xsm.at[4], xrm.at[4], dev(i, t, oh))
    m_swap.start()

    sw2.wait_recv()
    acc2[...] = acc2[...] + s2r[...].astype(F32)
    s3s[...] = acc2[:, 1].astype(BF16)
    sw3 = rcopy(s3s, s3r, qs.at[4], qr.at[4], dev(i_far, t))
    sw3.start()
    sv3.wait_recv()
    accu[0] = accu[0] + u3r[...]
    u4s[...] = accu[0]

    combine(mine_rows, eor, True)
    m_swap.wait_recv()
    outs[...] = (resid[...] + cacc[...] + mor[...].astype(F32)).astype(BF16)
    o_swap = rcopy(outs, outr, xsm.at[5], xrm.at[5], dev(i, t, oh))
    o_swap.start()
    for m in range(z.own_img):
        out_o[h * z.own_img + m] = outs[pl.ds(m * RP, L), :]
        tg_o[h * z.own_img + m] = tgs[pl.ds(m * RP, L), :]

    sw3.wait_recv()
    acc2[:, 0] = acc2[:, 0] + s3r[...].astype(F32)
    s4s[...] = acc2[:, 0].astype(BF16)
    last = []
    for dt in range(1, T):
        tt = lax.rem(t + dt, T)
        rows = pl.ds(al(tt * WR, WR), WR)
        last.append(rcopy(s4s.at[:, rows, :], s4r.at[dt], qs.at[4 + 2 * dt], qr.at[4 + 2 * dt], dev(i, tt)))
        last.append(rcopy(u4s.at[rows, :], u4r.at[dt], qs.at[5 + 2 * dt], qr.at[5 + 2 * dt], dev(i, tt)))
    for c in last:
        c.start()
    for c in last:
        c.wait_recv()
    wfin, sfin = ref["wfin"], ref["sfin"]
    my_rows = pl.ds(al(t * WR, WR), WR)
    total = acc2[:, 0, my_rows, :]
    part = accu[0, my_rows, :]
    for dt in range(1, T):
        total = total + s4r[dt].astype(F32)
        part = part + u4r[dt]
    wfin[...] = total
    u5s[...] = part
    sv5 = rcopy(u5s, u5r, qs.at[12], qr.at[12], dev(i, t, oh))
    sv5.start()
    t_swap.wait_recv()
    o_swap.wait_recv()
    for m in range(z.own_img):
        out_o[oh * z.own_img + m] = outr[pl.ds(m * RP, L), :]
        tg_o[oh * z.own_img + m] = tgr[pl.ds(m * RP, L), :]
    sv5.wait_recv()
    sfin[...] = u5s[...] + u5r[...]

    def grads_in(e, _):
        pltpu.make_async_copy(ing.at[e], ing.at[e], vr.at[0, e]).wait()
        pltpu.make_async_copy(backg.at[e], backg.at[e], vr.at[1, e]).wait()
        return 0

    lax.fori_loop(0, z.home, grads_in, 0)

    def grads_out(ep, _):
        p = lax.rem(ep, PR)
        for di in range(I):
            a_in = vin.at[0, pl.ds(0, DQ), pl.ds(0, FS)]
            a_back = vback.at[0, pl.ds(0, FS), pl.ds(0, DQ)]
            if di == 0:

                @pl.when(p != pos)
                def _():
                    pltpu.make_async_copy(a_in, a_in, vs.at[0, ep * I]).wait()
                    pltpu.make_async_copy(a_back, a_back, vs.at[1, ep * I]).wait()

            else:
                pltpu.make_async_copy(a_in, a_in, vs.at[0, ep * I + di]).wait()
                pltpu.make_async_copy(a_back, a_back, vs.at[1, ep * I + di]).wait()
        return 0

    lax.fori_loop(0, ED * PR, grads_out, 0)

    def back_out(n, _):
        for dt in range(T):

            def one():
                for row, buf in ((0, sis), (1, eos)):
                    d = buf.at[:, 0]
                    pltpu.make_async_copy(d, d, rs.at[row, n * T + dt]).wait()
                pltpu.make_async_copy(ggs.at[0], ggs.at[0], rs.at[2, n * T + dt]).wait()

            if dt == 0:
                pl.when(n > 0)(one)
            else:
                one()
        return 0

    lax.fori_loop(0, I, back_out, 0)
    for c in g_moved[1:] + x_moved[1:] + gate_moved[1:]:
        c.wait_send()
    for c in first + [b_x, b_y, b_ys, b_c, b_cs, f_x, f_c, f_cs, f_c2, f_c3]:
        c.wait_send()
    for c in (x_swap, gg_swap, db_swap, t_swap, m_swap, o_swap, *sw1, sv1, sw2, sv3, sw3, sv5, *last):
        c.wait_send()


def call(z, tok, cot, rt, wpack, spack, win, wback):
    T, I, PR, A, ED, D = z.tensor, z.team_i, z.pair, z.halves, z.own_e, z.width
    OWN, ROWS, EC, DQ, WR = z.own, z.rows, z.ecols, z.dq, z.wrow
    team = z.team
    V, S = pltpu.VMEM, pltpu.SemaphoreType.DMA
    ins = ["tok", "cot", "rt", "wpack", "spack", "win", "wback"]
    outs = {
        "out_o": jax.ShapeDtypeStruct(tok.shape, BF16),
        "tg_o": jax.ShapeDtypeStruct(tok.shape, BF16),
        "wfin": jax.ShapeDtypeStruct((4, WR, EC), F32),
        "sfin": jax.ShapeDtypeStruct((WR, LANES), F32),
        "ing": jax.ShapeDtypeStruct(win.shape, BF16),
        "backg": jax.ShapeDtypeStruct(wback.shape, BF16),
    }
    heads_own = z.own_img * z.nh
    scratch = {
        "wall": V((4, D, D), BF16), "sall": V((D, LANES), BF16), "gains": V((8, D), F32),
        "xn2a": V((ROWS, D), BF16), "cota": V((ROWS, D), BF16), "rp": V((ROWS, LANES), F32),
        "xs": V((OWN, D), F32), "both": V((ROWS, LANES), BF16), "idc": V((ROWS, LANES), F32),
        "idr": V((LANES, ROWS), F32), "gs": V((z.home, CAP, D), BF16), "xsl": V((z.home, CAP, D), BF16),
        "vin": V((ED, D, z.ff), BF16), "vback": V((ED, z.ff, D), BF16),
        "xr": V((ED, team, CAP, D), BF16), "gr": V((ED, team, CAP, D), BF16), "gater": V((team, 8, LANES), F32),
        "xn1": V((OWN, D), BF16), "qkv": V((3, OWN, D), BF16), "mixed": V((OWN, D), BF16),
        "probs": V((heads_own, z.pad, z.pad), BF16), "resid": V((OWN, D), F32), "router": V((ROWS, LANES), F32),
        "gcol": V((ROWS, LANES), F32), "gsend": V((z.home // ED, 8, LANES), F32),
        "hid": V((ED, team * CAP, z.ff), BF16), "igs": V((ED, team * CAP, z.ff), BF16),
        "eoa": V((T * CAP, D), F32), "sia": V((T * CAP, D), F32),
        "eos": V((ED, team, CAP, D), BF16), "sis": V((ED, team, CAP, D), BF16), "ggs": V((team, 8, LANES), F32),
        "eor": V((A, z.home, CAP, D), BF16), "sir": V((A, z.home, CAP, D), BF16), "ggr": V((team, 8, LANES), F32),
        "gcols": V((T, LANES, LANES), F32), "gtile": V((T * CAP, D), BF16),
        "ggx": V((team, 8, LANES), F32), "cacc": V((OWN, D), F32), "dbs": V((OWN, D), BF16), "dbr": V((OWN, D), BF16),
        "ggacc": V((2, OWN, LANES), F32), "small": V((D, LANES), F32), "nrows": V((LANES, D), F32),
        "rgrad": V((OWN, D), F32), "mg": V((OWN, D), BF16), "pg": V((3, OWN, D), BF16),
        "s1r": V((2, 2, DQ, 2 * D), BF16),
        "s2s": V((4, 2, DQ, EC), BF16), "s2r": V((4, 2, DQ, EC), BF16),
        "s3s": V((4, DQ, EC), BF16), "s3r": V((4, DQ, EC), BF16),
        "s4s": V((4, DQ, EC), BF16), "s4r": V((T, 4, WR, EC), BF16),
        "u1s": V((2, DQ, LANES), F32), "u1r": V((2, DQ, LANES), F32),
        "u3s": V((DQ, LANES), F32), "u3r": V((DQ, LANES), F32),
        "u4s": V((DQ, LANES), F32), "u4r": V((T, WR, LANES), F32),
        "u5s": V((WR, LANES), F32), "u5r": V((WR, LANES), F32),
        "accu": V((2, DQ, LANES), F32), "acc2": V((4, 2, DQ, EC), F32),
        "tgs": V((OWN, D), BF16), "tgr": V((OWN, D), BF16), "mos": V((OWN, D), BF16), "mor": V((OWN, D), BF16),
        "outs": V((OWN, D), BF16), "outr": V((OWN, D), BF16),
        "ws": S((5, 4)), "wr": S((5, 4)), "wl": S((2,)), "es": S((2, I * PR)), "er": S((2, I * PR)),
        "ds": S((3, team)), "dr": S((3, team)), "rs": S((3, team)), "rr": S((3, team)),
        "vs": S((2, ED * PR * I)), "vr": S((2, z.home)), "xsm": S((6,)), "xrm": S((6,)), "qs": S((20,)), "qr": S((20,)),
    }
    vmem = pl.BlockSpec(memory_space=pltpu.VMEM)
    anyw = pl.BlockSpec(memory_space=pl.ANY)
    names = ins + list(outs) + list(scratch)
    return pl.pallas_call(
        functools.partial(kernel, z, names),
        out_shape=tuple(outs.values()),
        in_specs=[vmem] * 5 + [anyw] * 2,
        out_specs=(vmem,) * 4 + (anyw,) * 2,
        scratch_shapes=list(scratch.values()),
        compiler_params=pltpu.CompilerParams(collective_id=0, has_side_effects=True, vmem_limit_bytes=64 * 1024 * 1024 - 65536),
        name="block",
    )(tok, cot, rt, wpack, spack, win, wback)


def solution(mesh):
    def local(tokens, cotangent, w_qkv, w_out, w_router, norm_one, norm_two, w_in, w_back, routes):
        images, length, width = tokens.shape
        z = Sizes(mesh.shape, images, length, width, w_in.shape[0], w_in.shape[2])
        R = z.reps
        wpack = jnp.concatenate([w_qkv, jnp.transpose(w_out)[None]], axis=0)
        fill = jnp.zeros((w_router.shape[0], LANES - EXPERTS - 2), BF16)
        spack = jnp.concatenate([w_router, norm_one[:, None], norm_two[:, None], fill], axis=1)
        sets = None
        if R > 1:
            sets = [[a * R + b for b in range(R)] for a in range(z.team_i)]
            w_in = lax.all_gather(w_in, "fsdp", axis=1, tiled=True, axis_index_groups=sets)
            w_back = lax.all_gather(w_back, "fsdp", axis=2, tiled=True, axis_index_groups=sets)
            place = lax.axis_index("tensor") * z.wrow

            def quarter(w, axis):
                w = lax.all_gather(w, "tensor", axis=axis, tiled=True)
                w = lax.all_gather(w, "fsdp", axis=axis, tiled=True, axis_index_groups=sets)
                return lax.dynamic_slice_in_dim(w, place, z.wrow, axis)

            wpack, spack = quarter(wpack, 1), quarter(spack, 0)
        out, tgrad, wfin, sfin, ing, backg = call(z, tokens, cotangent, routes, wpack, spack, w_in, w_back)
        if R > 1:
            ing = lax.psum_scatter(ing, "fsdp", scatter_dimension=1, tiled=True, axis_index_groups=sets)
            backg = lax.psum_scatter(backg, "fsdp", scatter_dimension=2, tiled=True, axis_index_groups=sets)

            def shard(w, axis):
                w = lax.all_gather(w, "tensor", axis=axis, tiled=True)
                w = lax.psum_scatter(w, "fsdp", scatter_dimension=axis, tiled=True, axis_index_groups=sets)
                rows = w.shape[axis] // z.tensor
                return lax.dynamic_slice_in_dim(w, lax.axis_index("tensor") * rows, rows, axis)

            wfin, sfin = shard(wfin, 1), shard(sfin, 0)
        return (
            out,
            tgrad.astype(F32),
            wfin[:3],
            jnp.transpose(wfin[3]),
            sfin[:, :EXPERTS],
            sfin[:, EXPERTS],
            sfin[:, EXPERTS + 1],
            ing.astype(F32),
            backg.astype(F32),
        )

    rows = P(("fsdp", "tensor"), None, None)
    qkv = P(None, ("fsdp", "tensor"), "heads")
    proj = P("heads", ("fsdp", "tensor"))
    table = P(("fsdp", "tensor"), None)
    gain = P(("fsdp", "tensor"))
    first = P("heads", "fsdp", "tensor")
    second = P("heads", "tensor", "fsdp")
    return jax.shard_map(
        local,
        mesh=mesh,
        in_specs=(rows, rows, qkv, proj, table, gain, gain, first, second, rows),
        out_specs=(rows, rows, qkv, proj, table, gain, gain, first, second),
        check_vma=False,
    )
```

profile of v0, /device:TPU:0, one launch (start us, length us, event | category | flops | bytes accessed | tf_op | source)
XLA Modules:
  0.0 304.3 jit_solution(3496765037240004201)
XLA Ops:
  0.6 0.0 copy-start.3
  0.7 0.0 copy-start.7
  0.7 0.0 copy-start.6
  0.7 2.2 copy.28.refs_0_
  3.0 0.0 copy-done.3
  3.0 1.0 copy.29.refs_1_
  4.0 1.0 copy.30.refs_2_
  5.0 0.0 copy-done.5
  5.0 0.6 pad_maximum_fusion.refs_3_
  5.6 0.1 copy.26
  5.7 0.1 copy.27
  5.8 0.1 pad.3.clone
  5.9 0.7 maximum_maximum_fusion.refs_4_
  6.6 283.0 %block.1 = (bf16[4,197,512]{2,1,0:T(8,128)(2,1)}, bf16[4,197,512]{2,1,0:T(8,128)(2,1)}, f32[4,32,256]{2,1,0:T(8,128)}, f32[32,128]{1,0:T(8,128)}, bf16[16,128,51...) custom-call(bf16[4,197,512]{2,1,0:T(8,128)(2,1)} %copy.28.refs_0_, bf16[4,197,512]{2,1,0:T(8,128)(2,1)} %copy.29.refs_1_, ...), custom_call_target="tpu_custom_call" | custom-call | tf_op jit(solution)/shard_map/block/pallas_call | solution.py:814
  289.6 1.5 slice_reduce_fusion
  291.1 1.5 slice.15
  292.6 1.4 slice_bitcast_fusion
  294.0 4.3 %convert_element_type.10 = f32[16,128,512]{2,1,0:T(8,128)} convert(bf16[16,128,512]{2,1,0:T(8,128)(2,1)} %get-tuple-element.19) | non-fusion elementwise | flops 1048576 | bytes 6291456 | tf_op jit(solution)/shard_map/convert_element_type | solution.py:866
  298.4 2.4 convert_element_type.11
  300.8 1.6 copy.32
  302.4 0.0 copy-done.1
  302.4 1.3 copy.31
  303.7 0.0 copy-done.4
  303.7 0.6 copy.34
  (16 shorter events, 0.0 us)
Async XLA Ops:
  0.6 2.3 copy-start.3
  0.7 3.3 %copy-start.7 = (s32[4,197,2]{1,2,0:T(2,128)S(1)}, s32[4,197,2]{1,2,0:T(2,128)}, u32[]{:S(2)}) copy-start(s32[4,197,2]{1,2,0:T(2,128)} %param.19) | copy-start | bytes 18916
  0.7 4.3 %copy-start.6 = (bf16[256,32]{0,1:T(8,128)(2,1)S(1)}, bf16[256,32]{0,1:T(8,128)(2,1)}, u32[]{:S(2)}) copy-start(bf16[256,32]{0,1:T(8,128)(2,1)} %param.13) | copy-start | bytes 49156
  0.7 4.3 %copy-start.5 = (bf16[3,32,256]{2,1,0:T(8,128)(2,1)S(1)}, bf16[3,32,256]{2,1,0:T(8,128)(2,1)}, u32[]{:S(2)}) copy-start(bf16[3,32,256]{2,1,0:T(8,128)(2,1)} %param.12) | copy-start | bytes 147460
  0.7 4.9 %copy-start.9 = (bf16[32]{0:T(256)(128)(2,1)S(1)}, bf16[32]{0:T(256)(128)(2,1)}, u32[]{:S(2)}) copy-start(bf16[32]{0:T(256)(128)(2,1)} %param.15) | copy-start | bytes 196
  0.7 5.0 %copy-start.10 = (bf16[32]{0:T(256)(128)(2,1)S(1)}, bf16[32]{0:T(256)(128)(2,1)}, u32[]{:S(2)}) copy-start(bf16[32]{0:T(256)(128)(2,1)} %param.16) | copy-start | bytes 196
  0.7 5.2 %copy-start.8 = (bf16[32,32]{1,0:T(8,128)(2,1)S(1)}, bf16[32,32]{1,0:T(8,128)(2,1)}, u32[]{:S(2)}) copy-start(bf16[32,32]{1,0:T(8,128)(2,1)} %param.14) | copy-start | bytes 6148
  294.0 4.3 %copy-start = (bf16[16,512,128]{2,1,0:T(8,128)(2,1)S(1)}, bf16[16,512,128]{2,1,0:T(8,128)(2,1)}, u32[]{:S(2)}) copy-start(bf16[16,512,128]{2,1,0:T(8,128)(2,1)} %get-tuple-element.20) | copy-start | bytes 6291460
  298.4 2.4 copy-start.2
  300.8 1.6 copy-start.1
  300.8 2.9 copy-start.4
where the time goes:
time: 305 us; the launch traced here: 304 us
  Pallas kernels  283 us (93%)
  local copies, waits for them, and re-layouts  12.4 us (4%)
  other arithmetic  8.08 us (3%)
    pallas_call x1, Pallas kernels, call(): pl.pallas_call(functools.partial(kernel, z, names), out_shape=tuple(outs....  283 us
    unnamed x28, local copies, waits for them, and re-layouts  7.76 us

commit v1 on v0

--- a/solution.py
+++ b/solution.py
@@ -11,6 +11,7 @@
 EXPERTS = 32
 CAP = 64
 PAIR = 2
+EARLY = 2
 LANES = 128
 MESH = pl.DeviceIdType.MESH
 F32 = jnp.float32
@@ -142,101 +143,24 @@
     for c in own_w:
         c.start()
 
-    xn2a, cota, rp = ref["xn2a"], ref["cota"], ref["rp"]
-    xn2a[...] = jnp.zeros_like(xn2a)
-    cota[...] = jnp.zeros_like(cota)
-    rp[...] = jnp.full_like(rp, -1.0)
-    xs = ref["xs"]
-    xs[...] = jnp.zeros_like(xs)
-    for m in range(z.images):
-        cota[pl.ds(m * RP, L), :] = cot[m]
-        rp[pl.ds(m * RP, L), 0:2] = rt[m].astype(F32)
-    for m in range(z.own_img):
-        xs[pl.ds(m * RP, L), :] = tok[h * z.own_img + m].astype(F32)
-
-    lane_all = iota((ROWS, LANES), 1)
-    r0, r1 = rp[:, 0:1], rp[:, 1:2]
-    oh0 = jnp.where(r0 == lane_all, 1.0, 0.0)
-    oh1 = jnp.where(r1 == lane_all, 1.0, 0.0)
-    both = ref["both"]
-    both[...] = (oh0 + oh1).astype(BF16)
-    idc = ref["idc"]
-
-    def count(c, _):
-        at = pl.ds(al(c * LANES, LANES), LANES)
-        before = iota((LANES, ROWS), 1) < iota((LANES, ROWS), 0) + (c * LANES).astype(F32)
-        counted = mm(jnp.where(before, 1.0, 0.0).astype(BF16), both[...])
-        lane = iota((LANES, LANES), 1)
-        q0, q1 = rp[at, 0:1], rp[at, 1:2]
-        number = counted + lane * CAP
-        n0 = jnp.sum(jnp.where(q0 == lane, number, 0.0), axis=1, keepdims=True)
-        n1 = jnp.sum(jnp.where(q1 == lane, number, 0.0), axis=1, keepdims=True)
-        n0 = jnp.where(q0 < 0.0, -1.0, n0)
-        n1 = jnp.where(q1 < 0.0, -1.0, n1)
-        idc[at, :] = jnp.where(lane == 0.0, n0, jnp.where(lane == 1.0, n1, -1.0))
-        return 0
-
-    lax.fori_loop(0, ROWS // LANES, count, 0)
-    idr = ref["idr"]
-    idr[...] = jnp.transpose(idc[...])
-
-    gs, xsl = ref["gs"], ref["xsl"]
-
-    def dispatch(source, target):
-        def one(c, _):
-            slot = iota((LANES, ROWS), 0) + (c * LANES + h * z.slots).astype(F32)
-            pick = jnp.where(idr[0:1, :] == slot, 1.0, 0.0) + jnp.where(idr[1:2, :] == slot, 1.0, 0.0)
-            got = mm(pick.astype(BF16), source[...]).astype(BF16)
-            per = LANES // CAP
-            target[pl.ds(c * per, per)] = got.reshape(per, CAP, D)
-            return 0
-
-        lax.fori_loop(0, z.slots // LANES, one, 0)
-
-    dispatch(cota, gs)
-
-    for c in first:
-        c.wait_recv()
-    for c in own_w:
-        c.wait()
-    b_x = rcopy(block(wall, i, h), block(wall, i, h), ws.at[2, 0], wr.at[2, 0], dev(i, t, oh))
-    b_y = rcopy(block(wall, i, h), block(wall, i, h), ws.at[2, 1], wr.at[2, 1], dev(i_far, t))
-    b_ys = rcopy(srows(i), srows(i), ws.at[2, 2], wr.at[2, 2], dev(i_far, t))
-    b_c = rcopy(block(wall, i, h), block(wall, i, h), ws.at[2, 3], wr.at[2, 3], dev(i_core, t))
-    b_cs = rcopy(srows(i), srows(i), ws.at[3, 0], wr.at[3, 0], dev(i_core, t))
-    for c in (b_y, b_x, b_ys, b_c, b_cs):
-        c.start()
-    b_y.wait_recv()
-    f_x = rcopy(block(wall, i_far, h), block(wall, i_far, h), ws.at[3, 1], wr.at[3, 1], dev(i, t, oh))
-    f_x.start()
-    f_c = rcopy(block(wall, i_far, h), block(wall, i_far, h), ws.at[3, 2], wr.at[3, 2], dev(i_core, t))
-    f_c.start()
-    b_ys.wait_recv()
-    f_cs = rcopy(srows(i_far), srows(i_far), ws.at[3, 3], wr.at[3, 3], dev(i_core, t))
-    f_cs.start()
-    b_x.wait_recv()
-    f_c2 = rcopy(block(wall, i, oh), block(wall, i, oh), ws.at[4, 0], wr.at[4, 0], dev(i_core, t))
-    f_c2.start()
-
     vin, vback = ref["vin"], ref["vback"]
     es, er = ref["es"], ref["er"]
     moved = []
-    k = 0
-    for dp in range(PR):
-        for di in range(I):
+    for di in range(I):
+        for dp in range(PR):
+            k = di * PR + dp
             ii, pp = lax.rem(i + di, I), lax.rem(pos + dp, PR)
             them = pl.ds((ii * PR + pp) * ED, ED)
             to_in = vin.at[:, pl.ds(al(i * DQ, DQ), DQ), pl.ds(al(pos * FS, FS), FS)]
             to_back = vback.at[:, pl.ds(al(pos * FS, FS), FS), pl.ds(al(i * DQ, DQ), DQ)]
-            if di == 0 and dp == 0:
+            if k == 0:
                 moved.append(lcopy(win.at[them], to_in, er.at[0, 0]))
                 moved.append(lcopy(wback.at[them], to_back, er.at[1, 0]))
             else:
                 to = dev(ii, half * PR + pp)
                 moved.append(rcopy(win.at[them], to_in, es.at[0, k], er.at[0, k], to))
                 moved.append(rcopy(wback.at[them], to_back, es.at[1, k], er.at[1, k], to))
-            k += 1
-    for c in moved:
+    for c in moved[: 2 * PR]:
         c.start()
 
     xr, gr, gater = ref["xr"], ref["gr"], ref["gater"]
@@ -261,7 +185,94 @@
             c.start()
         return made
 
+    xn2a, cota, rp = ref["xn2a"], ref["cota"], ref["rp"]
+    xn2a[...] = jnp.zeros_like(xn2a)
+    cota[...] = jnp.zeros_like(cota)
+    rp[...] = jnp.full_like(rp, -1.0)
+    xs = ref["xs"]
+    xs[...] = jnp.zeros_like(xs)
+    for m in range(z.images):
+        cota[pl.ds(m * RP, L), :] = cot[m]
+        rp[pl.ds(m * RP, L), 0:2] = rt[m].astype(F32)
+    for m in range(z.own_img):
+        xs[pl.ds(m * RP, L), :] = tok[h * z.own_img + m].astype(F32)
+
+    lane_all = iota((ROWS, LANES), 1)
+    r0, r1 = rp[:, 0:1], rp[:, 1:2]
+    oh0 = jnp.where(r0 == lane_all, 1.0, 0.0)
+    oh1 = jnp.where(r1 == lane_all, 1.0, 0.0)
+    both = ref["both"]
+    both[...] = (oh0 + oh1).astype(BF16)
+    idc = ref["idc"]
+
+    def count(c, _):
+        at = pl.ds(al(c * LANES, LANES), LANES)
+        before = iota((LANES, ROWS), 1) < iota((LANES, ROWS), 0) + (c * LANES).astype(F32)
+        counted = mm(jnp.where(before, 1.0, 0.0).astype(BF16), both[...])
+        lane = iota((LANES, LANES), 1)
+        q0, q1 = rp[at, 0:1], rp[at, 1:2]
+        number = counted + lane * CAP
+        n0 = jnp.sum(jnp.where(q0 == lane, number, 0.0), axis=1, keepdims=True)
+        n1 = jnp.sum(jnp.where(q1 == lane, number, 0.0), axis=1, keepdims=True)
+        n0 = jnp.where(q0 < 0.0, -1.0, n0)
+        n1 = jnp.where(q1 < 0.0, -1.0, n1)
+        idc[at, :] = jnp.where(lane == 0.0, n0, jnp.where(lane == 1.0, n1, -1.0))
+        return 0
+
+    lax.fori_loop(0, ROWS // LANES, count, 0)
+    idr = ref["idr"]
+    idr[...] = jnp.transpose(idc[...])
+
+    gs, xsl = ref["gs"], ref["xsl"]
+
+    gsend = ref["gsend"]
+
+    def dispatch(source, target, gates=None):
+        def one(c, _):
+            slot = iota((LANES, ROWS), 0) + (c * LANES + h * z.slots).astype(F32)
+            in0, in1 = idr[0:1, :] == slot, idr[1:2, :] == slot
+            pick = jnp.where(in0, 1.0, 0.0) + jnp.where(in1, 1.0, 0.0)
+            got = mm(pick.astype(BF16), source[...]).astype(BF16)
+            per = LANES // CAP
+            target[pl.ds(c * per, per)] = got.reshape(per, CAP, D)
+            if gates is not None:
+                w = jnp.where(in0, gates[0:1, :], 0.0) + jnp.where(in1, gates[1:2, :], 0.0)
+                col = jnp.broadcast_to(jnp.sum(w, axis=1, keepdims=True), (LANES, LANES))
+                sub, lane = iota((LANES, LANES), 0), iota((LANES, LANES), 1)
+                for q in range(LANES // z.lw):
+                    here = jnp.logical_and(lane < z.lw, lane == sub - q * z.lw)
+                    line = jnp.sum(jnp.where(here, col, 0.0), axis=0, keepdims=True)
+                    gsend[c * (LANES // z.lw) + q] = jnp.broadcast_to(line, (8, LANES))
+            return 0
+
+        lax.fori_loop(0, z.slots // LANES, one, 0)
+
+    for c in first:
+        c.wait_recv()
+    for c in own_w:
+        c.wait()
+    b_x = rcopy(block(wall, i, h), block(wall, i, h), ws.at[2, 0], wr.at[2, 0], dev(i, t, oh))
+    b_y = rcopy(block(wall, i, h), block(wall, i, h), ws.at[2, 1], wr.at[2, 1], dev(i_far, t))
+    b_ys = rcopy(srows(i), srows(i), ws.at[2, 2], wr.at[2, 2], dev(i_far, t))
+    b_c = rcopy(block(wall, i, h), block(wall, i, h), ws.at[2, 3], wr.at[2, 3], dev(i_core, t))
+    b_cs = rcopy(srows(i), srows(i), ws.at[3, 0], wr.at[3, 0], dev(i_core, t))
+    for c in (b_y, b_x, b_ys, b_c, b_cs):
+        c.start()
+    for c in moved[2 * PR :]:
+        c.start()
+    dispatch(cota, gs)
     g_moved = spread(gs, gr, 0, False)
+    b_y.wait_recv()
+    f_x = rcopy(block(wall, i_far, h), block(wall, i_far, h), ws.at[3, 1], wr.at[3, 1], dev(i, t, oh))
+    f_x.start()
+    f_c = rcopy(block(wall, i_far, h), block(wall, i_far, h), ws.at[3, 2], wr.at[3, 2], dev(i_core, t))
+    f_c.start()
+    b_ys.wait_recv()
+    f_cs = rcopy(srows(i_far), srows(i_far), ws.at[3, 3], wr.at[3, 3], dev(i_core, t))
+    f_cs.start()
+    b_x.wait_recv()
+    f_c2 = rcopy(block(wall, i, oh), block(wall, i, oh), ws.at[4, 0], wr.at[4, 0], dev(i_core, t))
+    f_c2.start()
 
     f_x.wait_recv()
     f_c3 = rcopy(block(wall, i_far, oh), block(wall, i_far, oh), ws.at[4, 1], wr.at[4, 1], dev(i_core, t))
@@ -324,20 +335,11 @@
     g0 = jnp.sum(jnp.where(rp[:, 0:1] == lane_all, router[...], 0.0), axis=1, keepdims=True)
     g1 = jnp.sum(jnp.where(rp[:, 1:2] == lane_all, router[...], 0.0), axis=1, keepdims=True)
     gcol[...] = jnp.where(lane_all == 0.0, g0, g1)
-    dispatch(xn2a, xsl)
+    grow = ref["grow"]
+    grow[...] = jnp.transpose(gcol[...])
+    dispatch(xn2a, xsl, grow)
+    gate_moved = spread(gsend, gater, 2, True)
     x_moved = spread(xsl, xr, 1, False)
-    gsend = ref["gsend"]
-
-    def gate_row(c, _):
-        lane = lane_all + (c * z.lw + h * z.slots).astype(F32)
-        keep = lane_all < z.lw
-        w = jnp.where(jnp.logical_and(keep, idc[:, 0:1] == lane), gcol[:, 0:1], 0.0)
-        w = w + jnp.where(jnp.logical_and(keep, idc[:, 1:2] == lane), gcol[:, 1:2], 0.0)
-        gsend[c] = jnp.broadcast_to(jnp.sum(w, axis=0, keepdims=True), (8, LANES))
-        return 0
-
-    lax.fori_loop(0, z.home // ED, gate_row, 0)
-    gate_moved = spread(gsend, gater, 2, True)
 
     hid, igs, gtile = ref["hid"], ref["igs"], ref["gtile"]
     eoa, sia = ref["eoa"], ref["sia"]
@@ -409,8 +411,8 @@
             return 0
 
         lax.fori_loop(0, ED * PR, part, 0)
+        give_back(n, 2, ggs, ggr, True)
         give_back(n, 0, sis, sir, False)
-        give_back(n, 2, ggs, ggr, True)
         return 0
 
     def give_back(n, row, src, dst, whole):
@@ -437,12 +439,6 @@
 
     lax.fori_loop(0, I, tile, 0)
 
-    def give_eo(n, _):
-        give_back(n, 1, eos, eor, False)
-        return 0
-
-    lax.fori_loop(0, I, give_eo, 0)
-
     ing, backg = ref["ing"], ref["backg"]
     vs, vr = ref["vs"], ref["vr"]
 
@@ -451,6 +447,11 @@
         cols = pl.ds(al(p * FS, FS), FS)
         vin[e, :, cols] = mm_tn(xr[e].reshape(z.team * CAP, D), igs[e, :, cols]).astype(BF16)
         vback[e, cols, :] = mm_tn(hid[e, :, cols], gr[e].reshape(z.team * CAP, D)).astype(BF16)
+        return 0
+
+    def give_grad(ep, _):
+        e, p = ep // PR, lax.rem(ep, PR)
+        cols = pl.ds(al(p * FS, FS), FS)
         for di in range(I):
             ii = lax.rem(i + di, I)
             part_in = vin.at[e, pl.ds(al(ii * DQ, DQ), DQ), cols]
@@ -474,7 +475,22 @@
                 rcopy(part_back, to_back, vs.at[1, ep * I + di], vr.at[1, e0 + e], to).start()
         return 0
 
-    lax.fori_loop(0, ED * PR, weight_grad, 0)
+
+    early = ED * PR * EARLY // 4
+    lax.fori_loop(0, early, weight_grad, 0)
+    lax.fori_loop(0, early, give_grad, 0)
+    lax.fori_loop(early, ED * PR, weight_grad, 0)
+
+    def back_gone(row, buf, n):
+        for dt in range(T):
+
+            def one():
+                pltpu.make_async_copy(buf, buf, rs.at[row, n * T + dt]).wait()
+
+            if dt == 0:
+                pl.when(n > 0)(one)
+            else:
+                one()
 
     ggx = ref["ggx"]
     cacc = ref["cacc"]
@@ -499,6 +515,13 @@
     gg_swap = rcopy(ggr, ggx, xsm.at[1], xrm.at[1], dev(i, t, oh))
     gg_swap.start()
     wait_home(0, slot_view(sir))
+
+    def give_eo(n, _):
+        give_back(n, 1, eos, eor, False)
+        return 0
+
+    lax.fori_loop(0, I, give_eo, 0)
+
 
     CH = 256
 
@@ -624,8 +647,6 @@
     tgrad = rgrad[...] + norm_back(cacc[...] * gains[0:1, :], normed, spread_one)
     tgs, tgr = ref["tgs"], ref["tgr"]
     tgs[...] = tgrad.astype(BF16)
-    t_swap = rcopy(tgs, tgr, xsm.at[3], xrm.at[3], dev(i, t, oh))
-    t_swap.start()
     small[...] = small[...] + jnp.transpose(nrows[...])
     for b, ii in enumerate((i_core, i_diag)):
         u1s[b] = small[quarter(ii), :]
@@ -648,37 +669,21 @@
         accu[b] = small[quarter(ii), :] + u1r[b]
     sw2 = rcopy(s2s, s2r, qs.at[2], qr.at[2], dev(i, t, oh))
     sw2.start()
+    t_swap = rcopy(tgs, tgr, xsm.at[3], xrm.at[3], dev(i, t, oh))
+    t_swap.start()
     u3s[...] = accu[1]
     sv3 = rcopy(u3s, u3r, qs.at[3], qr.at[3], dev(i_far, t))
     sv3.start()
-
-    out_o, tg_o = ref["out_o"], ref["tg_o"]
-    mos, mor, outs, outr = ref["mos"], ref["mor"], ref["outs"], ref["outr"]
-    wait_home(1, slot_view(eor))
-    combine(other_rows, eor, True)
-    mos[...] = cacc[...].astype(BF16)
-    m_swap = rcopy(mos, mor, xsm.at[4], xrm.at[4], dev(i, t, oh))
-    m_swap.start()
 
     sw2.wait_recv()
     acc2[...] = acc2[...] + s2r[...].astype(F32)
     s3s[...] = acc2[:, 1].astype(BF16)
     sw3 = rcopy(s3s, s3r, qs.at[4], qr.at[4], dev(i_far, t))
     sw3.start()
+    sw3.wait_recv()
     sv3.wait_recv()
     accu[0] = accu[0] + u3r[...]
     u4s[...] = accu[0]
-
-    combine(mine_rows, eor, True)
-    m_swap.wait_recv()
-    outs[...] = (resid[...] + cacc[...] + mor[...].astype(F32)).astype(BF16)
-    o_swap = rcopy(outs, outr, xsm.at[5], xrm.at[5], dev(i, t, oh))
-    o_swap.start()
-    for m in range(z.own_img):
-        out_o[h * z.own_img + m] = outs[pl.ds(m * RP, L), :]
-        tg_o[h * z.own_img + m] = tgs[pl.ds(m * RP, L), :]
-
-    sw3.wait_recv()
     acc2[:, 0] = acc2[:, 0] + s3r[...].astype(F32)
     s4s[...] = acc2[:, 0].astype(BF16)
     last = []
@@ -689,6 +694,23 @@
         last.append(rcopy(u4s.at[rows, :], u4r.at[dt], qs.at[5 + 2 * dt], qr.at[5 + 2 * dt], dev(i, tt)))
     for c in last:
         c.start()
+    lax.fori_loop(early, ED * PR, give_grad, 0)
+
+    out_o, tg_o = ref["out_o"], ref["tg_o"]
+    mos, mor, outs, outr = ref["mos"], ref["mor"], ref["outs"], ref["outr"]
+    wait_home(1, slot_view(eor))
+    combine(other_rows, eor, True)
+    mos[...] = cacc[...].astype(BF16)
+    m_swap = rcopy(mos, mor, xsm.at[4], xrm.at[4], dev(i, t, oh))
+    m_swap.start()
+    combine(mine_rows, eor, True)
+    m_swap.wait_recv()
+    outs[...] = (resid[...] + cacc[...] + mor[...].astype(F32)).astype(BF16)
+    o_swap = rcopy(outs, outr, xsm.at[5], xrm.at[5], dev(i, t, oh))
+    o_swap.start()
+    for m in range(z.own_img):
+        out_o[h * z.own_img + m] = outs[pl.ds(m * RP, L), :]
+        tg_o[h * z.own_img + m] = tgs[pl.ds(m * RP, L), :]
     for c in last:
         c.wait_recv()
     wfin, sfin = ref["wfin"], ref["sfin"]
@@ -737,18 +759,9 @@
     lax.fori_loop(0, ED * PR, grads_out, 0)
 
     def back_out(n, _):
-        for dt in range(T):
-
-            def one():
-                for row, buf in ((0, sis), (1, eos)):
-                    d = buf.at[:, 0]
-                    pltpu.make_async_copy(d, d, rs.at[row, n * T + dt]).wait()
-                pltpu.make_async_copy(ggs.at[0], ggs.at[0], rs.at[2, n * T + dt]).wait()
-
-            if dt == 0:
-                pl.when(n > 0)(one)
-            else:
-                one()
+        back_gone(0, sis.at[:, 0], n)
+        back_gone(1, eos.at[:, 0], n)
+        back_gone(2, ggs.at[0], n)
         return 0
 
     lax.fori_loop(0, I, back_out, 0)
@@ -779,7 +792,7 @@
         "wall": V((4, D, D), BF16), "sall": V((D, LANES), BF16), "gains": V((8, D), F32),
         "xn2a": V((ROWS, D), BF16), "cota": V((ROWS, D), BF16), "rp": V((ROWS, LANES), F32),
         "xs": V((OWN, D), F32), "both": V((ROWS, LANES), BF16), "idc": V((ROWS, LANES), F32),
-        "idr": V((LANES, ROWS), F32), "gs": V((z.home, CAP, D), BF16), "xsl": V((z.home, CAP, D), BF16),
+        "idr": V((LANES, ROWS), F32), "grow": V((LANES, ROWS), F32), "gs": V((z.home, CAP, D), BF16), "xsl": V((z.home, CAP, D), BF16),
         "vin": V((ED, D, z.ff), BF16), "vback": V((ED, z.ff, D), BF16),
         "xr": V((ED, team, CAP, D), BF16), "gr": V((ED, team, CAP, D), BF16), "gater": V((team, 8, LANES), F32),
         "xn1": V((OWN, D), BF16), "qkv": V((3, OWN, D), BF16), "mixed": V((OWN, D), BF16),

time: 305 us -> 277 us (0.908)
  Pallas kernels: 283 us -> 255 us
    pallas_call x1, Pallas kernels: 283 us -> 255 us  [call(): pl.pallas_call(functools.partial(kernel, z, names), out_shape=tuple(outs....]
where the time goes in v1:
time: 277 us; the launch traced here: 276 us
  Pallas kernels  255 us (92%)
  local copies, waits for them, and re-layouts  12.4 us (4%)
  other arithmetic  8.08 us (3%)
    pallas_call x1, Pallas kernels, call(): pl.pallas_call(functools.partial(kernel, z, names), out_shape=tuple(outs....  255 us
    unnamed x28, local copies, waits for them, and re-layouts  7.76 us

profile of v1, /device:TPU:0, one launch (start us, length us, event | category | flops | bytes accessed | tf_op | source)
XLA Modules:
  0.0 276.3 jit_solution(17858820629620125550)
XLA Ops:
  0.6 0.0 copy-start.3
  0.7 0.0 copy-start.7
  0.7 0.0 copy-start.6
  0.7 0.0 copy-start.5
  0.7 0.0 copy-start.9
  0.7 2.2 copy.28.refs_0_
  3.0 1.0 copy.29.refs_1_
  4.0 0.0 copy-done.7
  4.0 1.0 copy.30.refs_2_
  5.0 0.6 pad_maximum_fusion.refs_3_
  5.6 0.1 copy.26
  5.7 0.1 copy.27
  5.8 0.1 pad.3.clone
  5.9 0.7 maximum_maximum_fusion.refs_4_
  6.6 255.0 %block.1 = (bf16[4,197,512]{2,1,0:T(8,128)(2,1)}, bf16[4,197,512]{2,1,0:T(8,128)(2,1)}, f32[4,32,256]{2,1,0:T(8,128)}, f32[32,128]{1,0:T(8,128)}, bf16[16,128,51...) custom-call(bf16[4,197,512]{2,1,0:T(8,128)(2,1)} %copy.28.refs_0_, bf16[4,197,512]{2,1,0:T(8,128)(2,1)} %copy.29.refs_1_, ...), custom_call_target="tpu_custom_call" | custom-call | tf_op jit(solution)/shard_map/block/pallas_call | solution.py:827
  261.6 1.5 slice_reduce_fusion
  263.1 1.5 slice.15
  264.6 1.4 slice_bitcast_fusion
  266.0 4.3 %convert_element_type.10 = f32[16,128,512]{2,1,0:T(8,128)} convert(bf16[16,128,512]{2,1,0:T(8,128)(2,1)} %get-tuple-element.19) | non-fusion elementwise | flops 1048576 | bytes 6291456 | tf_op jit(solution)/shard_map/convert_element_type | solution.py:879
  270.3 0.0 copy-done
  270.3 2.4 convert_element_type.11
  272.8 1.6 copy.32
  274.4 1.3 copy.31
  275.7 0.6 copy.34
  (16 shorter events, 0.0 us)
Async XLA Ops:
  0.6 2.3 copy-start.3
  0.7 3.3 %copy-start.7 = (s32[4,197,2]{1,2,0:T(2,128)S(1)}, s32[4,197,2]{1,2,0:T(2,128)}, u32[]{:S(2)}) copy-start(s32[4,197,2]{1,2,0:T(2,128)} %param.19) | copy-start | bytes 18916
  0.7 4.3 %copy-start.6 = (bf16[256,32]{0,1:T(8,128)(2,1)S(1)}, bf16[256,32]{0,1:T(8,128)(2,1)}, u32[]{:S(2)}) copy-start(bf16[256,32]{0,1:T(8,128)(2,1)} %param.13) | copy-start | bytes 49156
  0.7 4.3 %copy-start.5 = (bf16[3,32,256]{2,1,0:T(8,128)(2,1)S(1)}, bf16[3,32,256]{2,1,0:T(8,128)(2,1)}, u32[]{:S(2)}) copy-start(bf16[3,32,256]{2,1,0:T(8,128)(2,1)} %param.12) | copy-start | bytes 147460
  0.7 4.9 %copy-start.9 = (bf16[32]{0:T(256)(128)(2,1)S(1)}, bf16[32]{0:T(256)(128)(2,1)}, u32[]{:S(2)}) copy-start(bf16[32]{0:T(256)(128)(2,1)} %param.15) | copy-start | bytes 196
  0.7 5.0 %copy-start.10 = (bf16[32]{0:T(256)(128)(2,1)S(1)}, bf16[32]{0:T(256)(128)(2,1)}, u32[]{:S(2)}) copy-start(bf16[32]{0:T(256)(128)(2,1)} %param.16) | copy-start | bytes 196
  0.7 5.2 %copy-start.8 = (bf16[32,32]{1,0:T(8,128)(2,1)S(1)}, bf16[32,32]{1,0:T(8,128)(2,1)}, u32[]{:S(2)}) copy-start(bf16[32,32]{1,0:T(8,128)(2,1)} %param.14) | copy-start | bytes 6148
  266.0 4.3 %copy-start = (bf16[16,512,128]{2,1,0:T(8,128)(2,1)S(1)}, bf16[16,512,128]{2,1,0:T(8,128)(2,1)}, u32[]{:S(2)}) copy-start(bf16[16,512,128]{2,1,0:T(8,128)(2,1)} %get-tuple-element.20) | copy-start | bytes 6291460
  270.3 2.4 copy-start.2
  272.8 1.6 copy-start.1
  272.8 2.9 %copy-start.4 = (f32[32,128]{1,0:T(8,128)S(1)}, f32[32,128]{1,0:T(8,128)}, u32[]{:S(2)}) copy-start(f32[32,128]{1,0:T(8,128)} %get-tuple-element.18) | copy-start | bytes 49156

commit v2 on v1

--- a/solution.py
+++ b/solution.py
@@ -77,7 +77,8 @@
 
 def kernel(z, names, *refs):
     ref = dict(zip(names, refs))
-    tok, cot, rt, wpack, spack = ref["tok"], ref["cot"], ref["rt"], ref["wpack"], ref["spack"]
+    tok, cot, rt, wqkv, wout = ref["tok"], ref["cot"], ref["rt"], ref["wqkv"], ref["wout"]
+    spack = ref["spack"]
     win, wback = ref["win"], ref["wback"]
     T, I, R = z.tensor, z.team_i, z.reps
     D, L, RP = z.width, z.length, z.pad
@@ -109,6 +110,18 @@
     def al(v, m):
         return pl.multiple_of(v, m)
 
+    tokv, cotv, ls = ref["tokv"], ref["cotv"], ref["ls"]
+    fetched = [lcopy(cot, cotv, ls.at[0]), lcopy(tok, tokv, ls.at[1])]
+    for c in fetched:
+        c.start()
+
+    turn = iota((WR, WR), 0) == iota((WR, WR), 1)
+    spack[...] = jnp.zeros_like(spack)
+    spack[:, 0:EXPERTS] = ref["table"][...]
+    for k, gain in enumerate((ref["one"], ref["two"])):
+        col = jnp.sum(jnp.where(turn, gain[...].astype(F32), 0.0), axis=1, keepdims=True)
+        spack[:, EXPERTS + k : EXPERTS + k + 1] = col.astype(BF16)
+
     bar = pltpu.get_barrier_semaphore()
     for di in range(I):
         for dt in range(T):
@@ -122,8 +135,8 @@
     wall, sall = ref["wall"], ref["sall"]
     ws, wr, wl = ref["ws"], ref["wr"], ref["wl"]
 
-    def shard_of(buf):
-        return buf.at[:, pl.ds(al(mine * WR, WR), WR), pl.ds(al(h * EC, LANES), EC)]
+    shard = (pl.ds(al(mine * WR, WR), WR), pl.ds(al(h * EC, LANES), EC))
+    qkv_shard, out_shard = wall.at[(pl.ds(0, 3), *shard)], wall.at[(3, *shard)]
 
     def block(buf, ii, hh):
         return buf.at[:, pl.ds(al(ii * DQ, DQ), DQ), pl.ds(al(hh * EC, LANES), EC)]
@@ -135,11 +148,12 @@
     first = []
     for dt in range(1, T):
         to = dev(i, lax.rem(t + dt, T))
-        first.append(rcopy(wpack, shard_of(wall), ws.at[0, dt], wr.at[0, dt], to))
+        first.append(rcopy(wqkv, qkv_shard, ws.at[0, dt], wr.at[0, dt], to))
+        first.append(rcopy(wout, out_shard, ws.at[5, dt], wr.at[5, dt], to))
         first.append(rcopy(spack, s_mine, ws.at[1, dt], wr.at[1, dt], to))
     for c in first:
         c.start()
-    own_w = [lcopy(wpack, shard_of(wall), wl.at[0]), lcopy(spack, s_mine, wl.at[1])]
+    own_w = [lcopy(wqkv, qkv_shard, wl.at[0]), lcopy(spack, s_mine, wl.at[1]), lcopy(wout, out_shard, wl.at[2])]
     for c in own_w:
         c.start()
 
@@ -191,11 +205,20 @@
     rp[...] = jnp.full_like(rp, -1.0)
     xs = ref["xs"]
     xs[...] = jnp.zeros_like(xs)
+    rtt = ref["rtt"]
     for m in range(z.images):
-        cota[pl.ds(m * RP, L), :] = cot[m]
-        rp[pl.ds(m * RP, L), 0:2] = rt[m].astype(F32)
+        rtt[...] = jnp.full_like(rtt, -1.0)
+        rtt[0:2, 0:L] = rt[m].astype(F32)
+        rp[pl.ds(m * RP, L), :] = jnp.transpose(rtt[...])[:L, :]
+    for c in fetched:
+        c.wait()
+    for m in range(z.images):
+        cota[pl.ds(m * RP, L), :] = cotv[:, m, :]
     for m in range(z.own_img):
-        xs[pl.ds(m * RP, L), :] = tok[h * z.own_img + m].astype(F32)
+        row = tokv[:, m, :].astype(F32)
+        for hh in range(1, z.heads):
+            row = jnp.where(h == hh, tokv[:, hh * z.own_img + m, :].astype(F32), row)
+        xs[pl.ds(m * RP, L), :] = row
 
     lane_all = iota((ROWS, LANES), 1)
     r0, r1 = rp[:, 0:1], rp[:, 1:2]
@@ -645,7 +668,7 @@
     normed, spread_one = norm_of(xs[...])
     nrows[EXPERTS : EXPERTS + 1, :] = jnp.sum(cacc[...] * normed, axis=0, keepdims=True)
     tgrad = rgrad[...] + norm_back(cacc[...] * gains[0:1, :], normed, spread_one)
-    tgs, tgr = ref["tgs"], ref["tgr"]
+    tgs, tg_p, out_p = ref["tgs"], ref["tg_p"], ref["out_p"]
     tgs[...] = tgrad.astype(BF16)
     small[...] = small[...] + jnp.transpose(nrows[...])
     for b, ii in enumerate((i_core, i_diag)):
@@ -669,8 +692,10 @@
         accu[b] = small[quarter(ii), :] + u1r[b]
     sw2 = rcopy(s2s, s2r, qs.at[2], qr.at[2], dev(i, t, oh))
     sw2.start()
-    t_swap = rcopy(tgs, tgr, xsm.at[3], xrm.at[3], dev(i, t, oh))
+    t_swap = rcopy(tgs, tg_p.at[mine_rows], xsm.at[3], xrm.at[3], dev(i, t, oh))
+    t_own = lcopy(tgs, tg_p.at[mine_rows], ls.at[2])
     t_swap.start()
+    t_own.start()
     u3s[...] = accu[1]
     sv3 = rcopy(u3s, u3r, qs.at[3], qr.at[3], dev(i_far, t))
     sv3.start()
@@ -696,8 +721,7 @@
         c.start()
     lax.fori_loop(early, ED * PR, give_grad, 0)
 
-    out_o, tg_o = ref["out_o"], ref["tg_o"]
-    mos, mor, outs, outr = ref["mos"], ref["mor"], ref["outs"], ref["outr"]
+    mos, mor, outs = ref["mos"], ref["mor"], ref["outs"]
     wait_home(1, slot_view(eor))
     combine(other_rows, eor, True)
     mos[...] = cacc[...].astype(BF16)
@@ -706,11 +730,10 @@
     combine(mine_rows, eor, True)
     m_swap.wait_recv()
     outs[...] = (resid[...] + cacc[...] + mor[...].astype(F32)).astype(BF16)
-    o_swap = rcopy(outs, outr, xsm.at[5], xrm.at[5], dev(i, t, oh))
+    o_swap = rcopy(outs, out_p.at[mine_rows], xsm.at[5], xrm.at[5], dev(i, t, oh))
+    o_own = lcopy(outs, out_p.at[mine_rows], ls.at[3])
     o_swap.start()
-    for m in range(z.own_img):
-        out_o[h * z.own_img + m] = outs[pl.ds(m * RP, L), :]
-        tg_o[h * z.own_img + m] = tgs[pl.ds(m * RP, L), :]
+    o_own.start()
     for c in last:
         c.wait_recv()
     wfin, sfin = ref["wfin"], ref["sfin"]
@@ -720,17 +743,21 @@
     for dt in range(1, T):
         total = total + s4r[dt].astype(F32)
         part = part + u4r[dt]
-    wfin[...] = total
+    wfs, sfs = ref["wfs"], ref["sfs"]
+    wfs[...] = total
+    w_own = lcopy(wfs, wfin, ls.at[4])
+    w_own.start()
     u5s[...] = part
     sv5 = rcopy(u5s, u5r, qs.at[12], qr.at[12], dev(i, t, oh))
     sv5.start()
     t_swap.wait_recv()
     o_swap.wait_recv()
-    for m in range(z.own_img):
-        out_o[oh * z.own_img + m] = outr[pl.ds(m * RP, L), :]
-        tg_o[oh * z.own_img + m] = tgr[pl.ds(m * RP, L), :]
+    t_own.wait()
+    o_own.wait()
     sv5.wait_recv()
-    sfin[...] = u5s[...] + u5r[...]
+    sfs[...] = u5s[...] + u5r[...]
+    s_own = lcopy(sfs, sfin, ls.at[5])
+    s_own.start()
 
     def grads_in(e, _):
         pltpu.make_async_copy(ing.at[e], ing.at[e], vr.at[0, e]).wait()
@@ -765,6 +792,8 @@
         return 0
 
     lax.fori_loop(0, I, back_out, 0)
+    w_own.wait()
+    s_own.wait()
     for c in g_moved[1:] + x_moved[1:] + gate_moved[1:]:
         c.wait_send()
     for c in first + [b_x, b_y, b_ys, b_c, b_cs, f_x, f_c, f_cs, f_c2, f_c3]:
@@ -773,22 +802,30 @@
         c.wait_send()
 
 
-def call(z, tok, cot, rt, wpack, spack, win, wback):
+def call(z, tok, cot, rt, wqkv, wout, table, one, two, win, wback):
     T, I, PR, A, ED, D = z.tensor, z.team_i, z.pair, z.halves, z.own_e, z.width
     OWN, ROWS, EC, DQ, WR = z.own, z.rows, z.ecols, z.dq, z.wrow
     team = z.team
     V, S = pltpu.VMEM, pltpu.SemaphoreType.DMA
-    ins = ["tok", "cot", "rt", "wpack", "spack", "win", "wback"]
+    ins = ["tok", "cot", "rt", "wqkv", "wout", "table", "one", "two", "win", "wback"]
     outs = {
-        "out_o": jax.ShapeDtypeStruct(tok.shape, BF16),
-        "tg_o": jax.ShapeDtypeStruct(tok.shape, BF16),
+        "out_p": jax.ShapeDtypeStruct((z.all, D), BF16),
+        "tg_p": jax.ShapeDtypeStruct((z.all, D), BF16),
         "wfin": jax.ShapeDtypeStruct((4, WR, EC), F32),
         "sfin": jax.ShapeDtypeStruct((WR, LANES), F32),
         "ing": jax.ShapeDtypeStruct(win.shape, BF16),
         "backg": jax.ShapeDtypeStruct(wback.shape, BF16),
     }
     heads_own = z.own_img * z.nh
+    wide = -(-z.length // LANES) * LANES
     scratch = {
+        "spack": V((WR, LANES), BF16),
+        "wfs": V((4, WR, EC), F32),
+        "sfs": V((WR, LANES), F32),
+        "tokv": V(tok.shape, BF16),
+        "cotv": V(cot.shape, BF16),
+        "rtt": V((LANES, wide), F32),
+        "ls": S((6,)),
         "wall": V((4, D, D), BF16), "sall": V((D, LANES), BF16), "gains": V((8, D), F32),
         "xn2a": V((ROWS, D), BF16), "cota": V((ROWS, D), BF16), "rp": V((ROWS, LANES), F32),
         "xs": V((OWN, D), F32), "both": V((ROWS, LANES), BF16), "idc": V((ROWS, LANES), F32),
@@ -815,9 +852,9 @@
         "u4s": V((DQ, LANES), F32), "u4r": V((T, WR, LANES), F32),
         "u5s": V((WR, LANES), F32), "u5r": V((WR, LANES), F32),
         "accu": V((2, DQ, LANES), F32), "acc2": V((4, 2, DQ, EC), F32),
-        "tgs": V((OWN, D), BF16), "tgr": V((OWN, D), BF16), "mos": V((OWN, D), BF16), "mor": V((OWN, D), BF16),
-        "outs": V((OWN, D), BF16), "outr": V((OWN, D), BF16),
-        "ws": S((5, 4)), "wr": S((5, 4)), "wl": S((2,)), "es": S((2, I * PR)), "er": S((2, I * PR)),
+        "tgs": V((OWN, D), BF16),  "mos": V((OWN, D), BF16), "mor": V((OWN, D), BF16),
+        "outs": V((OWN, D), BF16),
+        "ws": S((6, 4)), "wr": S((6, 4)), "wl": S((3,)), "es": S((2, I * PR)), "er": S((2, I * PR)),
         "ds": S((3, team)), "dr": S((3, team)), "rs": S((3, team)), "rr": S((3, team)),
         "vs": S((2, ED * PR * I)), "vr": S((2, z.home)), "xsm": S((6,)), "xrm": S((6,)), "qs": S((20,)), "qr": S((20,)),
     }
@@ -827,12 +864,69 @@
     return pl.pallas_call(
         functools.partial(kernel, z, names),
         out_shape=tuple(outs.values()),
-        in_specs=[vmem] * 5 + [anyw] * 2,
-        out_specs=(vmem,) * 4 + (anyw,) * 2,
+        in_specs=[anyw] * 2 + [vmem] * 6 + [anyw] * 2,
+        out_specs=(anyw,) * 6,
         scratch_shapes=list(scratch.values()),
         compiler_params=pltpu.CompilerParams(collective_id=0, has_side_effects=True, vmem_limit_bytes=64 * 1024 * 1024 - 65536),
         name="block",
-    )(tok, cot, rt, wpack, spack, win, wback)
+    )(tok, cot, rt, wqkv, wout, table, one, two, win, wback)
+
+
+def finish_kernel(z, out_p, tg_p, wfin, sfin, ing, backg, out, tgrad, qkv, proj, table, one, two, gin, gback, mix):
+    gin[...] = ing[...].astype(F32)
+    gback[...] = backg[...].astype(F32)
+
+    @pl.when(pl.program_id(0) == 0)
+    def _():
+        for m in range(z.images):
+            mix[:, m, :] = out_p[pl.ds(m * z.pad, z.length), :].astype(F32)
+        out[...] = mix[...].astype(BF16)
+        qkv[...] = wfin[0:3]
+        proj[...] = wfin[3]
+
+    @pl.when(pl.program_id(0) == 1)
+    def _():
+        for m in range(z.images):
+            tgrad[:, m, :] = tg_p[pl.ds(m * z.pad, z.length), :].astype(F32)
+        table[...] = sfin[:, 0:EXPERTS]
+        n = sfin.shape[0]
+        eye = iota((n, n), 0) == iota((n, n), 1)
+        for k, target in enumerate((one, two)):
+            col = sfin[:, EXPERTS + k : EXPERTS + k + 1]
+            target[...] = jnp.sum(jnp.where(eye, col, 0.0), axis=0, keepdims=True)
+
+
+def finish(z, out_p, tg_p, wfin, sfin, ing, backg):
+    steps = 4
+    part = z.home // steps
+    whole = pl.BlockSpec(memory_space=pltpu.VMEM)
+
+    def cut(a):
+        return pl.BlockSpec((part, *a.shape[1:]), lambda n: (n, 0, 0))
+
+    mixed = (z.length, z.images, z.width)
+    n = sfin.shape[0]
+    outs = (
+        jax.ShapeDtypeStruct(mixed, BF16),
+        jax.ShapeDtypeStruct(mixed, F32),
+        jax.ShapeDtypeStruct((3, *wfin.shape[1:]), F32),
+        jax.ShapeDtypeStruct(wfin.shape[1:], F32),
+        jax.ShapeDtypeStruct((n, EXPERTS), F32),
+        jax.ShapeDtypeStruct((1, n), F32),
+        jax.ShapeDtypeStruct((1, n), F32),
+        jax.ShapeDtypeStruct(ing.shape, F32),
+        jax.ShapeDtypeStruct(backg.shape, F32),
+    )
+    return pl.pallas_call(
+        functools.partial(finish_kernel, z),
+        grid=(steps,),
+        out_shape=outs,
+        in_specs=[whole] * 4 + [cut(ing), cut(backg)],
+        out_specs=(whole,) * 7 + (cut(ing), cut(backg)),
+        scratch_shapes=[pltpu.VMEM(mixed, F32)],
+        compiler_params=pltpu.CompilerParams(vmem_limit_bytes=64 * 1024 * 1024 - 65536),
+        name="finish",
+    )(out_p, tg_p, wfin, sfin, ing, backg)
 
 
 def solution(mesh):
@@ -840,9 +934,8 @@
         images, length, width = tokens.shape
         z = Sizes(mesh.shape, images, length, width, w_in.shape[0], w_in.shape[2])
         R = z.reps
-        wpack = jnp.concatenate([w_qkv, jnp.transpose(w_out)[None]], axis=0)
-        fill = jnp.zeros((w_router.shape[0], LANES - EXPERTS - 2), BF16)
-        spack = jnp.concatenate([w_router, norm_one[:, None], norm_two[:, None], fill], axis=1)
+        wqkv, wout, table = w_qkv, jnp.transpose(w_out), w_router
+        one, two = norm_one, norm_two
         sets = None
         if R > 1:
             sets = [[a * R + b for b in range(R)] for a in range(z.team_i)]
@@ -855,8 +948,11 @@
                 w = lax.all_gather(w, "fsdp", axis=axis, tiled=True, axis_index_groups=sets)
                 return lax.dynamic_slice_in_dim(w, place, z.wrow, axis)
 
-            wpack, spack = quarter(wpack, 1), quarter(spack, 0)
-        out, tgrad, wfin, sfin, ing, backg = call(z, tokens, cotangent, routes, wpack, spack, w_in, w_back)
+            wqkv, wout, table = quarter(wqkv, 1), quarter(wout, 0), quarter(table, 0)
+            one, two = quarter(one, 0), quarter(two, 0)
+        tok, cot = jnp.transpose(tokens, (1, 0, 2)), jnp.transpose(cotangent, (1, 0, 2))
+        rt = jnp.transpose(routes, (0, 2, 1))
+        out_p, tg_p, wfin, sfin, ing, backg = call(z, tok, cot, rt, wqkv, wout, table, one[None], two[None], w_in, w_back)
         if R > 1:
             ing = lax.psum_scatter(ing, "fsdp", scatter_dimension=1, tiled=True, axis_index_groups=sets)
             backg = lax.psum_scatter(backg, "fsdp", scatter_dimension=2, tiled=True, axis_index_groups=sets)
@@ -868,16 +964,17 @@
                 return lax.dynamic_slice_in_dim(w, lax.axis_index("tensor") * rows, rows, axis)
 
             wfin, sfin = shard(wfin, 1), shard(sfin, 0)
+        out, tgrad, qkv, proj, table, one, two, gin, gback = finish(z, out_p, tg_p, wfin, sfin, ing, backg)
         return (
-            out,
-            tgrad.astype(F32),
-            wfin[:3],
-            jnp.transpose(wfin[3]),
-            sfin[:, :EXPERTS],
-            sfin[:, EXPERTS],
-            sfin[:, EXPERTS + 1],
-            ing.astype(F32),
-            backg.astype(F32),
+            jnp.transpose(out, (1, 0, 2)),
+            jnp.transpose(tgrad, (1, 0, 2)),
+            qkv,
+            jnp.transpose(proj),
+            table,
+            one.reshape(-1),
+            two.reshape(-1),
+            gin,
+            gback,
         )
 
     rows = P(("fsdp", "tensor"), None, None)

time: 277 us -> 262 us (0.946)
  local copies, waits for them, and re-layouts: 12.4 us -> 0 us
  other arithmetic: 8.08 us -> 0 us
  Pallas kernels: 255 us -> 261 us
    pallas_call x0 -> x1, Pallas kernels: none -> 7.99 us  [finish(): pl.pallas_call(functools.partial(finish_kernel, z), grid=(steps,), out_sh...]
    unnamed x28 -> x0, local copies, waits for them, and re-layouts: 7.76 us -> none
    convert_element_type x2 -> x0, other arithmetic: 6.76 us -> none  [the longest x1 4.32 us: local(): ing.astype(F32)]
    slice x2 -> x0, local copies, waits for them, and re-layouts: 3.04 us -> none  [the longest x1 1.54 us: local(): wfin[:3]]
where the time goes in v2:
time: 262 us
  Pallas kernels  261 us (100%)
    pallas_call x1, Pallas kernels, call(): pl.pallas_call(functools.partial(kernel, z, names), out_shape=tuple(outs....  253 us
    pallas_call x1, Pallas kernels, finish(): pl.pallas_call(functools.partial(finish_kernel, z), grid=(steps,), out_sh...  7.99 us

profile of v2, /device:TPU:0, one launch (start us, length us, event | category | flops | bytes accessed | tf_op | source)
XLA Modules:
  0.0 262.1 jit_solution(11298419784050337584)
XLA Ops:
  0.6 253.4 %block.1 = (bf16[832,512]{1,0:T(8,128)(2,1)}, bf16[832,512]{1,0:T(8,128)(2,1)}, f32[4,32,256]{2,1,0:T(8,128)}, f32[32,128]{1,0:T(8,128)}, bf16[16,128,512]{2,1,0:T(8,128)(2,1)}, /*index=5*/bf16[16,512,128]{2,1,0:T(8,128)(2,1)}) custom-call(bf16[197,4,512]{2,1,0:T(4,128)(2,1)} %bitcast.11, bf16[197,4,512]{2,1,0:T(4,128)(2,1)} %bitcast.12, ...), custom_call_target="tpu_custom_call" | custom-call | tf_op jit(solution)/shard_map/block/pallas_call | solution.py:864
  254.1 8.0 %finish.1 = (bf16[197,4,512]{2,1,0:T(4,128)(2,1)}, f32[197,4,512]{2,1,0:T(4,128)}, f32[3,32,256]{2,1,0:T(8,128)}, f32[32,256]{1,0:T(8,128)}, f32[32,32]{1,0:T(8,...) custom-call(bf16[832,512]{1,0:T(8,128)(2,1)} %get-tuple-element.24.out_p, ...), custom_call_target="tpu_custom_call" | custom-call | tf_op jit(solution)/shard_map/finish/pallas_call | solution.py:920

commit v3 on v2

--- a/solution.py
+++ b/solution.py
@@ -91,6 +91,7 @@
     oh = 1 - h
     pos, half = lax.rem(t, PR), t // PR
     e0 = (i * PR + pos) * ED
+    CROSS, SAME = tuple(range(PR, T)), tuple(range(PR - 1, -1, -1))
     i_core = i + 1 - 2 * lax.rem(i, 2)
     i_far = lax.rem(i + 2, I)
     i_diag = lax.rem(i_core + 2, I)
@@ -98,6 +99,12 @@
 
     def dev(ii, tt, hh=None):
         return {"fsdp": ii * R + r, "heads": h if hh is None else hh, "tensor": tt}
+
+    def onto(dt):
+        return lax.rem(half + dt // PR, A) * PR + lax.rem(pos + dt % PR, PR)
+
+    def whence(dt):
+        return lax.rem(half - dt // PR + A, A) * PR + lax.rem(pos - dt % PR + PR, PR)
 
     def rcopy(src, dst, ssem, rsem, target):
         return pltpu.make_async_remote_copy(
@@ -180,12 +187,12 @@
     xr, gr, gater = ref["xr"], ref["gr"], ref["gater"]
     ds, dr = ref["ds"], ref["dr"]
 
-    def spread(src, dst, row, whole):
+    def spread(src, dst, row, whole, dts):
         made = []
         for di in range(I):
-            for dt in range(T):
+            for dt in dts:
                 kk = di * T + dt
-                ii, tt = lax.rem(i + di, I), lax.rem(t + dt, T)
+                ii, tt = lax.rem(i + di, I), onto(dt)
                 pp = lax.rem(tt, PR)
                 if whole:
                     s, d = src.at[ii * PR + pp], dst.at[mine]
@@ -281,10 +288,11 @@
     b_cs = rcopy(srows(i), srows(i), ws.at[3, 0], wr.at[3, 0], dev(i_core, t))
     for c in (b_y, b_x, b_ys, b_c, b_cs):
         c.start()
+    dispatch(cota, gs)
+    g_moved = spread(gs, gr, 0, False, CROSS)
     for c in moved[2 * PR :]:
         c.start()
-    dispatch(cota, gs)
-    g_moved = spread(gs, gr, 0, False)
+    g_moved += spread(gs, gr, 0, False, SAME)
     b_y.wait_recv()
     f_x = rcopy(block(wall, i_far, h), block(wall, i_far, h), ws.at[3, 1], wr.at[3, 1], dev(i, t, oh))
     f_x.start()
@@ -361,8 +369,8 @@
     grow = ref["grow"]
     grow[...] = jnp.transpose(gcol[...])
     dispatch(xn2a, xsl, grow)
-    gate_moved = spread(gsend, gater, 2, True)
-    x_moved = spread(xsl, xr, 1, False)
+    gate_moved = spread(gsend, gater, 2, True, CROSS + SAME)
+    x_moved = spread(xsl, xr, 1, False, CROSS + SAME)
 
     hid, igs, gtile = ref["hid"], ref["igs"], ref["gtile"]
     eoa, sia = ref["eoa"], ref["sia"]
@@ -383,7 +391,7 @@
         gi = lax.rem(i - n + I, I)
         grp = pl.ds(gi * T, T)
         for dt in range(T):
-            src = gi * T + lax.rem(t - dt + T, T)
+            src = gi * T + whence(dt)
             wait_role(0, n * T + dt, gr.at[:, src])
             wait_role(1, n * T + dt, xr.at[:, src])
             wait_role(2, n * T + dt, gater.at[src])
@@ -440,8 +448,8 @@
 
     def give_back(n, row, src, dst, whole):
         gi = lax.rem(i - n + I, I)
-        for dt in range(T):
-            tt = lax.rem(t + dt, T)
+        for dt in CROSS + SAME:
+            tt = onto(dt)
             kk = n * T + dt
             if whole:
                 s, d = src.at[gi * T + tt], dst.at[mine]
@@ -519,7 +527,7 @@
     cacc = ref["cacc"]
 
     def from_of(n, dt):
-        return lax.rem(i + n, I), lax.rem(t - dt + T, T)
+        return lax.rem(i + n, I), whence(dt)
 
     def wait_home(row, view):
         def one(n, _):
@@ -725,14 +733,20 @@
     wait_home(1, slot_view(eor))
     combine(other_rows, eor, True)
     mos[...] = cacc[...].astype(BF16)
-    m_swap = rcopy(mos, mor, xsm.at[4], xrm.at[4], dev(i, t, oh))
-    m_swap.start()
+    pieces = [pl.ds(m * RP, RP) for m in range(z.own_img)]
+    m_swap = []
+    for m, rows in enumerate(pieces):
+        m_swap.append(rcopy(mos.at[rows], mor.at[rows], xsm.at[4 + 2 * m], xrm.at[4 + 2 * m], dev(i, t, oh)))
+        m_swap[m].start()
     combine(mine_rows, eor, True)
-    m_swap.wait_recv()
-    outs[...] = (resid[...] + cacc[...] + mor[...].astype(F32)).astype(BF16)
-    o_swap = rcopy(outs, out_p.at[mine_rows], xsm.at[5], xrm.at[5], dev(i, t, oh))
+    o_swap = []
+    for m, rows in enumerate(pieces):
+        m_swap[m].wait_recv()
+        outs[rows, :] = (resid[rows, :] + cacc[rows, :] + mor[rows, :].astype(F32)).astype(BF16)
+        there = out_p.at[pl.ds(al(h * OWN + m * RP, 16), RP)]
+        o_swap.append(rcopy(outs.at[rows], there, xsm.at[5 + 2 * m], xrm.at[5 + 2 * m], dev(i, t, oh)))
+        o_swap[m].start()
     o_own = lcopy(outs, out_p.at[mine_rows], ls.at[3])
-    o_swap.start()
     o_own.start()
     for c in last:
         c.wait_recv()
@@ -751,7 +765,8 @@
     sv5 = rcopy(u5s, u5r, qs.at[12], qr.at[12], dev(i, t, oh))
     sv5.start()
     t_swap.wait_recv()
-    o_swap.wait_recv()
+    for c in o_swap:
+        c.wait_recv()
     t_own.wait()
     o_own.wait()
     sv5.wait_recv()
@@ -794,11 +809,12 @@
     lax.fori_loop(0, I, back_out, 0)
     w_own.wait()
     s_own.wait()
-    for c in g_moved[1:] + x_moved[1:] + gate_moved[1:]:
-        c.wait_send()
+    for c in g_moved + x_moved + gate_moved:
+        if c.is_remote:
+            c.wait_send()
     for c in first + [b_x, b_y, b_ys, b_c, b_cs, f_x, f_c, f_cs, f_c2, f_c3]:
         c.wait_send()
-    for c in (x_swap, gg_swap, db_swap, t_swap, m_swap, o_swap, *sw1, sv1, sw2, sv3, sw3, sv5, *last):
+    for c in (x_swap, gg_swap, db_swap, t_swap, *m_swap, *o_swap, *sw1, sv1, sw2, sv3, sw3, sv5, *last):
         c.wait_send()
 
 
@@ -856,7 +872,7 @@
         "outs": V((OWN, D), BF16),
         "ws": S((6, 4)), "wr": S((6, 4)), "wl": S((3,)), "es": S((2, I * PR)), "er": S((2, I * PR)),
         "ds": S((3, team)), "dr": S((3, team)), "rs": S((3, team)), "rr": S((3, team)),
-        "vs": S((2, ED * PR * I)), "vr": S((2, z.home)), "xsm": S((6,)), "xrm": S((6,)), "qs": S((20,)), "qr": S((20,)),
+        "vs": S((2, ED * PR * I)), "vr": S((2, z.home)), "xsm": S((4 + 2 * z.own_img,)), "xrm": S((4 + 2 * z.own_img,)), "qs": S((20,)), "qr": S((20,)),
     }
     vmem = pl.BlockSpec(memory_space=pltpu.VMEM)
     anyw = pl.BlockSpec(memory_space=pl.ANY)
@@ -872,38 +888,60 @@
     )(tok, cot, rt, wqkv, wout, table, one, two, win, wback)
 
 
-def finish_kernel(z, out_p, tg_p, wfin, sfin, ing, backg, out, tgrad, qkv, proj, table, one, two, gin, gback, mix):
-    gin[...] = ing[...].astype(F32)
-    gback[...] = backg[...].astype(F32)
-
-    @pl.when(pl.program_id(0) == 0)
-    def _():
-        for m in range(z.images):
-            mix[:, m, :] = out_p[pl.ds(m * z.pad, z.length), :].astype(F32)
-        out[...] = mix[...].astype(BF16)
-        qkv[...] = wfin[0:3]
-        proj[...] = wfin[3]
-
-    @pl.when(pl.program_id(0) == 1)
-    def _():
-        for m in range(z.images):
-            tgrad[:, m, :] = tg_p[pl.ds(m * z.pad, z.length), :].astype(F32)
-        table[...] = sfin[:, 0:EXPERTS]
-        n = sfin.shape[0]
-        eye = iota((n, n), 0) == iota((n, n), 1)
-        for k, target in enumerate((one, two)):
-            col = sfin[:, EXPERTS + k : EXPERTS + k + 1]
-            target[...] = jnp.sum(jnp.where(eye, col, 0.0), axis=0, keepdims=True)
+def finish_kernel(z, parts, out_p, tg_p, wfin, sfin, ing, backg, out, tgrad, qkv, proj, table, one, two, gin, gback, *work):
+    half_in, half_back, full_in, full_back, outl, tgl, outv, tgv, mix, got, put = work
+    step = z.home // parts
+    cuts = [pl.ds(p * step, step) for p in range(parts)]
+    tasks = [(ing, half_in, full_in, gin), (backg, half_back, full_back, gback)]
+    reads, writes = [], []
+    for p, cut in enumerate(cuts):
+        for k, (src, low, full, dst) in enumerate(tasks):
+            reads.append(pltpu.make_async_copy(src.at[cut], low.at[cut], got.at[k, p]))
+            writes.append(pltpu.make_async_copy(full.at[cut], dst.at[cut], put.at[k, p]))
+    rows = [pltpu.make_async_copy(out_p, outl, got.at[0, parts]), pltpu.make_async_copy(tg_p, tgl, got.at[1, parts])]
+    for c in reads[:2] + rows + reads[2:]:
+        c.start()
+
+    def convert(p):
+        for k, (_, low, full, _) in enumerate(tasks):
+            reads[2 * p + k].wait()
+            full[cuts[p]] = low[cuts[p]].astype(F32)
+            writes[2 * p + k].start()
+
+    last = [
+        pltpu.make_async_copy(outv, out, put.at[0, parts]),
+        pltpu.make_async_copy(tgv, tgrad, put.at[1, parts]),
+    ]
+    convert(0)
+    rows[0].wait()
+    for m in range(z.images):
+        mix[:, m, :] = outl[pl.ds(m * z.pad, z.length), :].astype(F32)
+    outv[...] = mix[...].astype(BF16)
+    last[0].start()
+    convert(1)
+    rows[1].wait()
+    for m in range(z.images):
+        tgv[:, m, :] = tgl[pl.ds(m * z.pad, z.length), :].astype(F32)
+    last[1].start()
+    for p in range(2, parts):
+        convert(p)
+    qkv[...] = wfin[0:3]
+    proj[...] = wfin[3]
+    table[...] = sfin[:, 0:EXPERTS]
+    n = sfin.shape[0]
+    eye = iota((n, n), 0) == iota((n, n), 1)
+    for k, target in enumerate((one, two)):
+        col = sfin[:, EXPERTS + k : EXPERTS + k + 1]
+        target[...] = jnp.sum(jnp.where(eye, col, 0.0), axis=0, keepdims=True)
+    for c in writes + last:
+        c.wait()
 
 
 def finish(z, out_p, tg_p, wfin, sfin, ing, backg):
-    steps = 4
-    part = z.home // steps
+    parts = 4
+    V, S = pltpu.VMEM, pltpu.SemaphoreType.DMA
     whole = pl.BlockSpec(memory_space=pltpu.VMEM)
-
-    def cut(a):
-        return pl.BlockSpec((part, *a.shape[1:]), lambda n: (n, 0, 0))
-
+    anyw = pl.BlockSpec(memory_space=pl.ANY)
     mixed = (z.length, z.images, z.width)
     n = sfin.shape[0]
     outs = (
@@ -917,13 +955,15 @@
         jax.ShapeDtypeStruct(ing.shape, F32),
         jax.ShapeDtypeStruct(backg.shape, F32),
     )
+    scratch = [V(ing.shape, BF16), V(backg.shape, BF16), V(ing.shape, F32), V(backg.shape, F32)]
+    scratch += [V(out_p.shape, BF16), V(tg_p.shape, BF16), V(mixed, BF16), V(mixed, F32), V(mixed, F32)]
+    scratch += [S((2, parts + 1)), S((2, parts + 1))]
     return pl.pallas_call(
-        functools.partial(finish_kernel, z),
-        grid=(steps,),
+        functools.partial(finish_kernel, z, parts),
         out_shape=outs,
-        in_specs=[whole] * 4 + [cut(ing), cut(backg)],
-        out_specs=(whole,) * 7 + (cut(ing), cut(backg)),
-        scratch_shapes=[pltpu.VMEM(mixed, F32)],
+        in_specs=[anyw] * 2 + [whole] * 2 + [anyw] * 2,
+        out_specs=(anyw,) * 2 + (whole,) * 5 + (anyw,) * 2,
+        scratch_shapes=scratch,
         compiler_params=pltpu.CompilerParams(vmem_limit_bytes=64 * 1024 * 1024 - 65536),
         name="finish",
     )(out_p, tg_p, wfin, sfin, ing, backg)

time: 262 us -> 261 us (level)
  no operation moved by 1% of the time
where the time goes in v3:
time: 261 us; the launch traced here: 260 us
  Pallas kernels  259 us (99%)
    pallas_call x1, Pallas kernels, call(): pl.pallas_call(functools.partial(kernel, z, names), out_shape=tuple(outs....  252 us
    pallas_call x1, Pallas kernels, finish(): pl.pallas_call(functools.partial(finish_kernel, z, parts), out_shape=outs...  7.23 us

profile of v3, /device:TPU:0, one launch (start us, length us, event | category | flops | bytes accessed | tf_op | source)
XLA Modules:
  0.0 260.1 jit_solution(16064939784907688465)
XLA Ops:
  0.6 252.1 %block.1 = (bf16[832,512]{1,0:T(8,128)(2,1)}, bf16[832,512]{1,0:T(8,128)(2,1)}, f32[4,32,256]{2,1,0:T(8,128)}, f32[32,128]{1,0:T(8,128)}, bf16[16,128,512]{2,1,0:T(8,128)(2,1)}, /*index=5*/bf16[16,512,128]{2,1,0:T(8,128)(2,1)}) custom-call(bf16[197,4,512]{2,1,0:T(4,128)(2,1)} %bitcast.11, bf16[197,4,512]{2,1,0:T(4,128)(2,1)} %bitcast.12, ...), custom_call_target="tpu_custom_call" | custom-call | tf_op jit(solution)/shard_map/block/pallas_call | solution.py:880
  252.8 7.2 %finish.1 = (bf16[197,4,512]{2,1,0:T(4,128)(2,1)}, f32[197,4,512]{2,1,0:T(4,128)}, f32[3,32,256]{2,1,0:T(8,128)}, f32[32,256]{1,0:T(8,128)}, f32[32,32]{1,0:T(8,...) custom-call(bf16[832,512]{1,0:T(8,128)(2,1)} %get-tuple-element.24.out_p, ...), custom_call_target="tpu_custom_call" | custom-call | tf_op jit(solution)/shard_map/finish/pallas_call | solution.py:961
